TPU v7x, 32 devices: a whole 2x2x4 slice. The times are simulated.
32 devices in a mesh: tri: 32 (over z, y, x, core).
Axes of the slice: x: 2, y: 2, z: 4, core: 2. Of those that a mesh axis runs over, the one named last changes fastest.
Arguments:
- amplitudes: bfloat16 [32, 2816, 5632], P('tri'), as said below
- factors: bfloat16 [22528, 1280], P('tri'), may hold values from -2.5 to 2.5
- occ_energy: float32 [44], replicated, may hold values from -3 to -0.5
- virt_energy: float32 [512], replicated, may hold values from 0.2 to 6
Outputs:
- new_amplitudes: float32 [32, 2816, 5632], P('tri')
Inputs may be any that keep to these rules, and one draw needn't show every extreme that they name: `amplitudes`: the matrix T assembled from the tiles is symmetric.
All inputs are finite; a program needn't handle non-finite values.
Results may differ from a plain program's by a relative error of at most 0.0069.
Values may be sent and summed in bfloat16 or wider, within the bound.
A program may use at most 192 MiB of HBM per device.

v0:
```python
import functools

import jax
import jax.numpy as jnp
from jax import lax
from jax.experimental import pallas as pl
from jax.experimental.pallas import tpu as pltpu
from jax.sharding import PartitionSpec as P


STRIPES = 8
SIDES = 2
PLACES = STRIPES // SIDES
VMEM = 60 * 2**20


def send(value, target):
    count = lax.axis_size("tri")
    return lax.ppermute(value, "tri", [(source, target(source)) for source in range(count)])


def set_gather(own, band_size):
    def along(step):
        def target(source):
            stripe, column = source // band_size, source % band_size
            place, side = stripe // SIDES, stripe % SIDES
            return ((place + step) % PLACES * SIDES + side) * band_size + column

        return target

    def across(source):
        return source // band_size * band_size ^ band_size | source % band_size

    near = [own] + [send(own, along(step)) for step in range(1, PLACES)]
    far = [send(piece, across) for piece in near]
    return near, far


def row_block(rows):
    block = rows
    while block > 352 and block % 32 == 0:
        block //= 2
    return block


def fill(held, pieces, place, side, rows, units):
    near, far = pieces
    for near_ref, far_ref, unit in zip(near, far, units):
        at = 0 if len(units) == 1 else lax.rem(place - unit + PLACES, PLACES) * SIDES
        for ref, part in ((near_ref, side), (far_ref, 1 - side)):
            held[pl.ds(pl.multiple_of((at + part) * rows, 16), rows), :] = ref[...]


def terms_kernel(rows, steps, where_ref, tile_ref, *refs):
    near, far = refs[:PLACES], refs[PLACES : 2 * PLACES]
    sent_ref, kept_ref, held = refs[2 * PLACES :]
    step = pl.program_id(0)

    @pl.when(step == 0)
    def _():
        fill(held, (near, far), where_ref[0], where_ref[1], rows, range(PLACES))

    product = jnp.dot(tile_ref[0], held[...], preferred_element_type=jnp.float32)
    product = product.astype(sent_ref.dtype)

    @pl.when(step < steps)
    def _():
        sent_ref[0] = product

    @pl.when(step >= steps)
    def _():
        kept_ref[0] = product


def image_terms(amplitudes, pieces, where, half, band_size):
    near, far = pieces
    rows, width = near[0].shape
    columns = amplitudes.shape[2]
    block = row_block(rows)
    parts = rows // block
    pairs = band_size // 4
    steps = pairs * parts

    def tile_index(step, where_ref):
        top, low = where_ref[2], where_ref[3]
        top = top if half else 1 - top
        second = step // steps
        place = step % steps // parts * 2 + jnp.where(second == 0, 1 - low, low)
        return 0, (top * pairs * 2 + place) * parts + step % parts, 0

    def sent_index(step, where_ref):
        at = jnp.minimum(step, steps - 1)
        return at // parts, at % parts, 0

    def kept_index(step, where_ref):
        at = jnp.maximum(step - steps, 0)
        return at // parts, at % parts, 0

    whole = pl.BlockSpec((rows, width), lambda step, where_ref: (0, 0))
    out = jax.ShapeDtypeStruct((pairs, rows, width), jnp.bfloat16)
    return pl.pallas_call(
        functools.partial(terms_kernel, rows, steps),
        out_shape=(out, out),
        grid_spec=pltpu.PrefetchScalarGridSpec(
            num_scalar_prefetch=1,
            grid=(2 * steps,),
            in_specs=[pl.BlockSpec((1, block, columns), tile_index)] + [whole] * (2 * PLACES),
            out_specs=(
                pl.BlockSpec((1, block, width), sent_index),
                pl.BlockSpec((1, block, width), kept_index),
            ),
            scratch_shapes=[pltpu.VMEM((columns, width), jnp.bfloat16)],
        ),
        compiler_params=pltpu.CompilerParams(vmem_limit_bytes=VMEM),
        cost_estimate=pl.CostEstimate(
            flops=4 * steps * block * columns * width,
            bytes_accessed=4 * steps * block * columns,
            transcendentals=0,
        ),
    )(where, amplitudes, *near, *far)


def half_reduce(sent, kept, device, levels):
    received = send(sent, lambda source: source ^ 1)
    buffer = kept.astype(jnp.float32) + received.astype(jnp.float32)
    for level in range(1, levels):
        pairs = buffer.reshape(-1, 2, *buffer.shape[1:])
        bit = device // 2**level % 2
        keeping = lax.dynamic_index_in_dim(pairs, bit, 1, keepdims=False)
        outgoing = lax.dynamic_index_in_dim(pairs, 1 - bit, 1, keepdims=False)
        received = send(outgoing.astype(jnp.bfloat16), lambda source: source ^ 2**level)
        buffer = keeping + received.astype(jnp.float32)
    return buffer[0]


def band_gather(own, device, levels):
    rows, width = own.shape
    buffer = own[None]
    for level in reversed(range(levels)):
        received = send(buffer, lambda source: source ^ 2**level)
        bit = device // 2**level % 2
        first = jnp.where(bit == 0, buffer, received)
        second = jnp.where(bit == 0, received, buffer)
        buffer = jnp.stack([first, second], 1).reshape(-1, rows, width)
    return buffer.reshape(-1, width)


def update_kernel(rows, units, parts, chained, where_ref, *refs):
    bands = refs[:parts]
    refs = refs[parts:]
    count = len(units)
    near = [refs[part * count : (part + 1) * count] for part in range(parts)]
    refs = refs[parts * count :]
    far = [refs[part * count : (part + 1) * count] for part in range(parts)]
    refs = refs[parts * count :]
    row_ref, column_ref = refs[:2]
    refs = refs[2 + chained :]
    out_ref, held = refs[0], refs[1:]

    @pl.when(pl.program_id(0) == 0)
    def _():
        for part in range(parts):
            fill(held[part], (near[part], far[part]), where_ref[0], where_ref[1], rows, units)

    inner = None
    for part in range(parts):
        product = lax.dot_general(
            bands[part][...],
            held[part][...],
            (((1,), (1,)), ((), ())),
            preferred_element_type=jnp.float32,
        )
        inner = product if inner is None else inner + product
    out_ref[0] = -inner / (row_ref[...] + column_ref[0])


def update(bands, near, far, row_energy, column_energy, where, units, earlier):
    parts = len(bands)
    rows = near[0][0].shape[0]
    height = bands[0].shape[0]
    columns = STRIPES * rows
    span = len(units) * SIDES * rows
    block = row_block(rows)
    widths = [band.shape[1] for band in bands]

    def at(where_ref):
        return lax.rem(where_ref[0] - units[0] + PLACES, PLACES) if len(units) == 1 else 0

    chained = int(earlier is not None)
    held = [near[part][unit] for part in range(parts) for unit in units]
    held += [far[part][unit] for part in range(parts) for unit in units]
    in_specs = [pl.BlockSpec((block, width), lambda step, where_ref: (step, 0)) for width in widths]
    in_specs += [pl.BlockSpec(piece.shape, lambda step, where_ref: (0, 0)) for piece in held]
    in_specs += [
        pl.BlockSpec((block, 1), lambda step, where_ref: (step, 0)),
        pl.BlockSpec((1, 1, span), lambda step, where_ref: (at(where_ref), 0, 0)),
    ]
    operands = [where, *bands, *held, row_energy[:, None], column_energy.reshape(-1, 1, span)]
    aliases = {}
    if chained:
        aliases = {len(operands): 0}
        in_specs.append(pl.BlockSpec(memory_space=pl.ANY))
        operands.append(earlier)
    return pl.pallas_call(
        functools.partial(update_kernel, rows, units, parts, chained),
        out_shape=jax.ShapeDtypeStruct((1, height, columns), jnp.float32),
        grid_spec=pltpu.PrefetchScalarGridSpec(
            num_scalar_prefetch=1,
            grid=(height // block,),
            in_specs=in_specs,
            out_specs=pl.BlockSpec((1, block, span), lambda step, where_ref: (0, step, at(where_ref))),
            scratch_shapes=[pltpu.VMEM((span, width), jnp.bfloat16) for width in widths],
        ),
        input_output_aliases=aliases,
        compiler_params=pltpu.CompilerParams(vmem_limit_bytes=VMEM),
        cost_estimate=pl.CostEstimate(
            flops=2 * height * span * sum(widths),
            bytes_accessed=4 * height * span,
            transcendentals=0,
        ),
    )(*operands)


def part_bounds(naux):
    first = -(-naux // 512) * 256
    return [(0, first), (first, naux)]


def per_device(amplitudes, factors, occ_energy, virt_energy):
    device = lax.axis_index("tri")
    band_size = lax.axis_size("tri") // STRIPES
    levels = band_size.bit_length() - 1
    rows, naux = factors.shape
    stripe, column = device // band_size, device % band_size
    pair_energy = (virt_energy[None, :] - occ_energy[:, None]).reshape(-1)
    grid = pair_energy.reshape(STRIPES, band_size, rows)
    row_energy = lax.dynamic_index_in_dim(grid, stripe, 0, keepdims=False).reshape(-1)
    column_energy = lax.dynamic_index_in_dim(grid, column, 1, keepdims=False).reshape(-1)
    where = jnp.stack(
        [stripe // SIDES, stripe % SIDES, column // (band_size // 2), column % 2]
    ).astype(jnp.int32)

    bounds = part_bounds(naux)
    bands, near, far = [], [], []
    for start, end in bounds:
        own = factors[:, start:end]
        pieces = set_gather(own, band_size)
        halves = []
        for half in range(2):
            sent, kept = image_terms(amplitudes, pieces, where, half, band_size)
            halves.append(half_reduce(sent, kept, device, levels - 1))
        received = send(halves[0].astype(jnp.bfloat16), lambda source: source ^ band_size // 2)
        images = halves[1] + received.astype(jnp.float32) + own.astype(jnp.float32)
        dressed = images.astype(jnp.bfloat16)
        near_part, far_part = set_gather(dressed, band_size)
        near.append(near_part)
        far.append(far_part)
        bands.append(band_gather(dressed, device, levels))

    if rows * SIDES % 128:
        groups = [list(range(PLACES))]
    else:
        groups = [[unit] for unit in range(PLACES)]
    result = None
    for group in groups:
        result = update(bands, near, far, row_energy, column_energy, where, group, result)
    return result


def solution(mesh):
    placed = (P("tri", None, None), P("tri", None), P(), P())
    return jax.shard_map(
        per_device, mesh=mesh, in_specs=placed, out_specs=P("tri", None, None), check_vma=False
    )
```

profile of v0, /device:TPU:0, one launch (start us, length us, event | category | flops | bytes accessed | tf_op | source)
XLA Modules:
  0.0 638.5 jit_solution(17779270160096366973)
XLA Ops:
  10.5 83.8 %collective-permute-done.12.refs_1_ = bf16[704,512]{1,0:T(8,128)(2,1)S(1)} collective-permute-done((bf16[704,512]{1,0:T(8,128)(2,1)S(1)}, bf16[704,512]{1,0:T(8,128)(2,1)S(1)}, u32[]{:S(2)}, u32[]{:S(2)}) %collective-permute-start.12) | collective-permute-done | bytes 720928 | tf_op jit(solution)/shard_map/ppermute | solution.py:19
  98.5 49.1 %collective-permute-done.13.refs_2_ = bf16[704,512]{1,0:T(8,128)(2,1)} collective-permute-done((bf16[704,512]{1,0:T(8,128)(2,1)S(1)}, bf16[704,512]{1,0:T(8,128)(2,1)}, u32[]{:S(2)}, u32[]{:S(2)}) %collective-permute-start.13) | collective-permute-done | bytes 720928 | tf_op jit(solution)/shard_map/ppermute | solution.py:19
  149.7 16.0 %collective-permute-done.14.refs_3_ = bf16[704,512]{1,0:T(8,128)(2,1)} collective-permute-done((bf16[704,512]{1,0:T(8,128)(2,1)S(1)}, bf16[704,512]{1,0:T(8,128)(2,1)}, u32[]{:S(2)}, u32[]{:S(2)}) %collective-permute-start.14) | collective-permute-done | bytes 720928 | tf_op jit(solution)/shard_map/ppermute | solution.py:19
  169.8 21.2 %collective-permute-done.6.refs_7_ = bf16[704,768]{1,0:T(8,128)(2,1)} collective-permute-done((bf16[704,768]{1,0:T(8,128)(2,1)}, bf16[704,768]{1,0:T(8,128)(2,1)}, u32[]{:S(2)}, u32[]{:S(2)}) %collective-permute-start.6) | collective-permute-done | bytes 1081376 | tf_op jit(solution)/shard_map/ppermute | solution.py:19
  191.0 20.4 %shard_map.47 = (bf16[1,704,768]{2,1,0:T(8,128)(2,1)}, bf16[1,704,768]{2,1,0:T(8,128)(2,1)}) custom-call(s32[4]{0:T(128)} %pad_add_fusion.where_ref, bf16[1,2816,5632]{2,1,0:T(8,128)(2,1)} %tile_ref.7, bf16[704,768]{1,0:T(8,128)(2,1)} %slice.6.refs_0_, bf16[704,768]{1,0:T(8,128)(2,1)} %collective-permute-done.refs_1_, ...), custom_call_target="tpu_custom_call" | custom-call | flops 12180258816 | bytes 15859712 | tf_op jit(solution)/shard_map/pallas_call | solution.py:101
  211.4 20.4 %shard_map.46 = (bf16[1,704,768]{2,1,0:T(8,128)(2,1)}, bf16[1,704,768]{2,1,0:T(8,128)(2,1)}) custom-call(s32[4]{0:T(128)} %pad_add_fusion.where_ref, bf16[1,2816,5632]{2,1,0:T(8,128)(2,1)} %tile_ref.7, bf16[704,768]{1,0:T(8,128)(2,1)} %slice.6.refs_0_, bf16[704,768]{1,0:T(8,128)(2,1)} %collective-permute-done.refs_1_, ...), custom_call_target="tpu_custom_call" | custom-call | flops 12180258816 | bytes 15859712 | tf_op jit(solution)/shard_map/pallas_call | solution.py:101
  237.3 12.8 %collective-permute-done.18.refs_7_ = bf16[704,512]{1,0:T(8,128)(2,1)} collective-permute-done((bf16[704,512]{1,0:T(8,128)(2,1)}, bf16[704,512]{1,0:T(8,128)(2,1)}, u32[]{:S(2)}, u32[]{:S(2)}) %collective-permute-start.18) | collective-permute-done | bytes 720928 | tf_op jit(solution)/shard_map/ppermute | solution.py:19
  250.2 15.1 %shard_map.49 = (bf16[1,704,512]{2,1,0:T(8,128)(2,1)}, bf16[1,704,512]{2,1,0:T(8,128)(2,1)}) custom-call(s32[4]{0:T(128)} %pad_add_fusion.where_ref, bf16[1,2816,5632]{2,1,0:T(8,128)(2,1)} %tile_ref.7, bf16[704,512]{1,0:T(8,128)(2,1)} %copy-done.4, bf16[704,512]{1,0:T(8,128)(2,1)} %copy-done.5, bf16[704,512]{1,0:T(8,128)(2,1)} %collective-permute-done.13.refs_2_, ...), custom_call_target="tpu_custom_call" | custom-call | flops 8120172544 | bytes 15859712 | tf_op jit(solution)/shard_map/pallas_call | solution.py:101
  265.3 15.3 %shard_map.48 = (bf16[1,704,512]{2,1,0:T(8,128)(2,1)}, bf16[1,704,512]{2,1,0:T(8,128)(2,1)}) custom-call(s32[4]{0:T(128)} %pad_add_fusion.where_ref, bf16[1,2816,5632]{2,1,0:T(8,128)(2,1)} %tile_ref.7, bf16[704,512]{1,0:T(8,128)(2,1)} %copy-done.4, bf16[704,512]{1,0:T(8,128)(2,1)} %copy-done.5, bf16[704,512]{1,0:T(8,128)(2,1)} %collective-permute-done.13.refs_2_, ...), custom_call_target="tpu_custom_call" | custom-call | flops 8120172544 | bytes 15859712 | tf_op jit(solution)/shard_map/pallas_call | solution.py:101
  285.5 14.7 %collective-permute-done.21 = bf16[704,512]{1,0:T(8,128)(2,1)S(1)} collective-permute-done((bf16[704,512]{1,0:T(8,128)(2,1)S(1)}, bf16[704,512]{1,0:T(8,128)(2,1)S(1)}, u32[]{:S(2)}, u32[]{:S(2)}) %collective-permute-start.21) | collective-permute-done | bytes 720928 | tf_op jit(solution)/shard_map/ppermute | solution.py:19
  302.8 20.7 %collective-permute-done.10 = bf16[1,704,768]{2,1,0:T(8,128)(2,1)} collective-permute-done((bf16[1,704,768]{2,1,0:T(8,128)(2,1)S(1)}, bf16[1,704,768]{2,1,0:T(8,128)(2,1)}, u32[]{:S(2)}, u32[]{:S(2)}) %collective-permute-start.10) | collective-permute-done | bytes 1081376 | tf_op jit(solution)/shard_map/ppermute | solution.py:19
  326.4 11.7 %collective-permute-done.22 = bf16[1,704,512]{2,1,0:T(8,128)(2,1)} collective-permute-done((bf16[1,704,512]{2,1,0:T(8,128)(2,1)}, bf16[1,704,512]{2,1,0:T(8,128)(2,1)}, u32[]{:S(2)}, u32[]{:S(2)}) %collective-permute-start.22) | collective-permute-done | bytes 720928 | tf_op jit(solution)/shard_map/ppermute | solution.py:19
  342.3 37.2 %collective-permute-start.32 = (bf16[704,768]{1,0:T(8,128)(2,1)S(1)}, bf16[704,768]{1,0:T(8,128)(2,1)}, u32[]{:S(2)}, u32[]{:S(2)}) collective-permute-start(bf16[704,768]{1,0:T(8,128)(2,1)S(1)} %fusion.1.refs_2_), channel_id=1, source_target_pairs={{0,8},{1,9},{2,10},{3,11},{4,12},{5,13},{6,14},{7,15},{8,16},{9,17... | collective-permute-start | bytes 3244040 | tf_op jit(solution)/shard_map/ppermute | solution.py:19
  386.1 14.3 %collective-permute-start.28 = (bf16[704,768]{1,0:T(8,128)(2,1)S(1)}, bf16[704,768]{1,0:T(8,128)(2,1)}, u32[]{:S(2)}, u32[]{:S(2)}) collective-permute-start(bf16[704,768]{1,0:T(8,128)(2,1)S(1)} %fusion.1.refs_2_), channel_id=1, source_target_pairs={{0,16},{1,17},{2,18},{3,19},{4,20},{5,21},{6,22},{7,23},{8,24},{9,... | collective-permute-start | bytes 3244040 | tf_op jit(solution)/shard_map/ppermute | solution.py:19
  406.3 13.1 %collective-permute-done.33.refs_3_ = bf16[704,512]{1,0:T(8,128)(2,1)} collective-permute-done((bf16[704,512]{1,0:T(8,128)(2,1)}, bf16[704,512]{1,0:T(8,128)(2,1)}, u32[]{:S(2)}, u32[]{:S(2)}) %collective-permute-start.33) | collective-permute-done | bytes 720928 | tf_op jit(solution)/shard_map/ppermute | solution.py:19
  419.4 3.4 collective-permute-start.24
  426.0 54.4 %collective-permute-done.29.refs_3_ = bf16[704,512]{1,0:T(8,128)(2,1)S(1)} collective-permute-done((bf16[704,512]{1,0:T(8,128)(2,1)}, bf16[704,512]{1,0:T(8,128)(2,1)S(1)}, u32[]{:S(2)}, u32[]{:S(2)}) %collective-permute-start.29) | collective-permute-done | bytes 720928 | tf_op jit(solution)/shard_map/ppermute | solution.py:19
  480.4 43.9 %collective-permute-start.25 = (bf16[704,512]{1,0:T(8,128)(2,1)}, bf16[704,512]{1,0:T(8,128)(2,1)}, u32[]{:S(2)}, u32[]{:S(2)}) collective-permute-start(bf16[704,512]{1,0:T(8,128)(2,1)} %fusion.3.refs_3_), channel_id=1, source_target_pairs={{0,24},{1,25},{2,26},{3,27},{4,28},{5,29},{6,30},{7,31},{8,0},{9,1... | collective-permute-start | bytes 2162696 | tf_op jit(solution)/shard_map/ppermute | solution.py:19
  526.3 18.6 %shard_map.50.refs_8_ = f32[1,2816,5632]{2,1,0:T(8,128)} custom-call(s32[4]{0:T(128)} %pad_add_fusion.where_ref, bf16[2816,768]{1,0:T(8,128)(2,1)} %bitcast.56, bf16[2816,512]{1,0:T(8,128)(2,1)} %bitcast.60, bf16[704,768]{1,0:T(8,128)(2,1)} %copy-done, bf16[704,512]{1,0:T(8,128)(2,1)} %fusion.3.refs_3_, bf16[704,768]{1,0:T(8,128)(2,1)} %copy-done.10, ...), custom_call_target="tpu_custom_call" | custom-call | flops 10150215680 | bytes 15859712 | tf_op jit(solution)/shard_map/pallas_call | solution.py:204
  548.9 18.6 %shard_map.51.refs_8_ = f32[1,2816,5632]{2,1,0:T(8,128)} custom-call(s32[4]{0:T(128)} %pad_add_fusion.where_ref, bf16[2816,768]{1,0:T(8,128)(2,1)} %bitcast.57, bf16[2816,512]{1,0:T(8,128)(2,1)} %bitcast.61, bf16[704,768]{1,0:T(8,128)(2,1)} %collective-permute-done.32.refs_2_, ...), custom_call_target="tpu_custom_call", output_to_operand_aliasing={{}: (9, {})} | custom-call | flops 10150215680 | bytes 15859712 | tf_op jit(solution)/shard_map/pallas_call | solution.py:204
  567.6 14.6 %collective-permute-done.31.refs_5_ = bf16[704,512]{1,0:T(8,128)(2,1)} collective-permute-done((bf16[704,512]{1,0:T(8,128)(2,1)}, bf16[704,512]{1,0:T(8,128)(2,1)}, u32[]{:S(2)}, u32[]{:S(2)}) %collective-permute-start.31) | collective-permute-done | bytes 720928 | tf_op jit(solution)/shard_map/ppermute | solution.py:19
  582.2 18.7 %shard_map.52.refs_8_ = f32[1,2816,5632]{2,1,0:T(8,128)} custom-call(s32[4]{0:T(128)} %pad_add_fusion.where_ref, bf16[2816,768]{1,0:T(8,128)(2,1)} %bitcast.58, bf16[2816,512]{1,0:T(8,128)(2,1)} %bitcast.62, bf16[704,768]{1,0:T(8,128)(2,1)} %collective-permute-done.28.refs_2_, bf16[704,512]{1,0:T(8,128)(2,1)} %copy-done.11, ...), custom_call_target="tpu_custom_call", output_to_operand_aliasing={{}: (9, {})} | custom-call | flops 10150215680 | bytes 15859712 | tf_op jit(solution)/shard_map/pallas_call | solution.py:204
  600.9 18.0 %collective-permute-done.26.refs_4_ = bf16[704,768]{1,0:T(8,128)(2,1)S(1)} collective-permute-done((bf16[704,768]{1,0:T(8,128)(2,1)S(1)}, bf16[704,768]{1,0:T(8,128)(2,1)S(1)}, u32[]{:S(2)}, u32[]{:S(2)}) %collective-permute-start.26) | collective-permute-done | bytes 1081376 | tf_op jit(solution)/shard_map/ppermute | solution.py:19
  619.8 18.6 %shard_map.53 = f32[1,2816,5632]{2,1,0:T(8,128)} custom-call(s32[4]{0:T(128)} %pad_add_fusion.where_ref, bf16[2816,768]{1,0:T(8,128)(2,1)} %bitcast.59, bf16[2816,512]{1,0:T(8,128)(2,1)} %bitcast.63, bf16[704,768]{1,0:T(8,128)(2,1)} %copy-done.6, bf16[704,512]{1,0:T(8,128)(2,1)} %collective-permute-done.25.refs_3_, ...), custom_call_target="tpu_custom_call", output_to_operand_aliasing={{}: (9, {})} | custom-call | flops 10150215680 | bytes 15859712 | tf_op jit(solution)/shard_map/pallas_call | solution.py:204
  (115 shorter events, 63.6 us)
Async XLA Ops:
  2.4 93.7 %collective-permute-start = (bf16[704,768]{1,0:T(8,128)(2,1)}, bf16[704,768]{1,0:T(8,128)(2,1)}, u32[]{:S(2)}, u32[]{:S(2)}) collective-permute-start(bf16[704,768]{1,0:T(8,128)(2,1)} %slice.6.refs_0_), channel_id=1, source_target_pairs={{0,8},{1,9},{2,10},{3,11},{4,12},{5,13},{6,14},{7,15},{8,16},{9,17... | collective-permute-start | bytes 3244040 | tf_op jit(solution)/shard_map/ppermute | solution.py:19
  5.5 91.0 %collective-permute-start.1 = (bf16[704,768]{1,0:T(8,128)(2,1)}, bf16[704,768]{1,0:T(8,128)(2,1)}, u32[]{:S(2)}, u32[]{:S(2)}) collective-permute-start(bf16[704,768]{1,0:T(8,128)(2,1)} %slice.6.refs_0_), channel_id=1, source_target_pairs={{0,16},{1,17},{2,18},{3,19},{4,20},{5,21},{6,22},{7,23},{8,24},{9,... | collective-permute-start | bytes 3244040 | tf_op jit(solution)/shard_map/ppermute | solution.py:19
  8.1 90.1 %collective-permute-start.2 = (bf16[704,768]{1,0:T(8,128)(2,1)}, bf16[704,768]{1,0:T(8,128)(2,1)}, u32[]{:S(2)}, u32[]{:S(2)}) collective-permute-start(bf16[704,768]{1,0:T(8,128)(2,1)} %slice.6.refs_0_), channel_id=1, source_target_pairs={{0,24},{1,25},{2,26},{3,27},{4,28},{5,29},{6,30},{7,31},{8,0},{9,1... | collective-permute-start | bytes 3244040 | tf_op jit(solution)/shard_map/ppermute | solution.py:19
  9.5 84.9 %collective-permute-start.12 = (bf16[704,512]{1,0:T(8,128)(2,1)S(1)}, bf16[704,512]{1,0:T(8,128)(2,1)S(1)}, u32[]{:S(2)}, u32[]{:S(2)}) collective-permute-start(bf16[704,512]{1,0:T(8,128)(2,1)S(1)} %slice.7.refs_0_), channel_id=1, source_target_pairs={{0,8},{1,9},{2,10},{3,11},{4,12},{5,13},{6,14},{7,15},{8,16},{9,17... | collective-permute-start | bytes 2162696 | tf_op jit(solution)/shard_map/ppermute | solution.py:19
  10.2 137.4 %collective-permute-start.13 = (bf16[704,512]{1,0:T(8,128)(2,1)S(1)}, bf16[704,512]{1,0:T(8,128)(2,1)}, u32[]{:S(2)}, u32[]{:S(2)}) collective-permute-start(bf16[704,512]{1,0:T(8,128)(2,1)S(1)} %slice.7.refs_0_), channel_id=1, source_target_pairs={{0,16},{1,17},{2,18},{3,19},{4,20},{5,21},{6,22},{7,23},{8,24},{9,... | collective-permute-start | bytes 2162696 | tf_op jit(solution)/shard_map/ppermute | solution.py:19
  94.4 72.9 %collective-permute-start.3 = (bf16[704,768]{1,0:T(8,128)(2,1)}, bf16[704,768]{1,0:T(8,128)(2,1)}, u32[]{:S(2)}, u32[]{:S(2)}) collective-permute-start(bf16[704,768]{1,0:T(8,128)(2,1)} %slice.6.refs_0_), channel_id=1, source_target_pairs={{0,4},{1,5},{2,6},{3,7},{4,0},{5,1},{6,2},{7,3},{8,12},{9,13},{10,... | collective-permute-start | bytes 3244040 | tf_op jit(solution)/shard_map/ppermute | solution.py:19
  96.1 71.6 %collective-permute-start.4 = (bf16[704,768]{1,0:T(8,128)(2,1)}, bf16[704,768]{1,0:T(8,128)(2,1)}, u32[]{:S(2)}, u32[]{:S(2)}) collective-permute-start(bf16[704,768]{1,0:T(8,128)(2,1)} %collective-permute-done.refs_1_), channel_id=1, source_target_pairs={{0,4},{1,5},{2,6},{3,7},{4,0},{5,1},{6,2},{7,3},{8,12},{9,13},{10,... | collective-permute-start | bytes 3244040 | tf_op jit(solution)/shard_map/ppermute | solution.py:19
  96.4 72.9 %collective-permute-start.5 = (bf16[704,768]{1,0:T(8,128)(2,1)}, bf16[704,768]{1,0:T(8,128)(2,1)}, u32[]{:S(2)}, u32[]{:S(2)}) collective-permute-start(bf16[704,768]{1,0:T(8,128)(2,1)} %collective-permute-done.1.refs_2_), channel_id=1, source_target_pairs={{0,4},{1,5},{2,6},{3,7},{4,0},{5,1},{6,2},{7,3},{8,12},{9,13},{10,... | collective-permute-start | bytes 3244040 | tf_op jit(solution)/shard_map/ppermute | solution.py:19
  98.2 92.8 %collective-permute-start.6 = (bf16[704,768]{1,0:T(8,128)(2,1)}, bf16[704,768]{1,0:T(8,128)(2,1)}, u32[]{:S(2)}, u32[]{:S(2)}) collective-permute-start(bf16[704,768]{1,0:T(8,128)(2,1)} %collective-permute-done.2.refs_3_), channel_id=1, source_target_pairs={{0,4},{1,5},{2,6},{3,7},{4,0},{5,1},{6,2},{7,3},{8,12},{9,13},{10,... | collective-permute-start | bytes 3244040 | tf_op jit(solution)/shard_map/ppermute | solution.py:19
  165.7 69.4 %collective-permute-start.15 = (bf16[704,512]{1,0:T(8,128)(2,1)S(1)}, bf16[704,512]{1,0:T(8,128)(2,1)}, u32[]{:S(2)}, u32[]{:S(2)}) collective-permute-start(bf16[704,512]{1,0:T(8,128)(2,1)S(1)} %slice.7.refs_0_), channel_id=1, source_target_pairs={{0,4},{1,5},{2,6},{3,7},{4,0},{5,1},{6,2},{7,3},{8,12},{9,13},{10,... | collective-permute-start | bytes 2162696 | tf_op jit(solution)/shard_map/ppermute | solution.py:19
  167.3 69.6 %collective-permute-start.16 = (bf16[704,512]{1,0:T(8,128)(2,1)S(1)}, bf16[704,512]{1,0:T(8,128)(2,1)}, u32[]{:S(2)}, u32[]{:S(2)}) collective-permute-start(bf16[704,512]{1,0:T(8,128)(2,1)S(1)} %collective-permute-done.12.refs_1_), channel_id=1, source_target_pairs={{0,4},{1,5},{2,6},{3,7},{4,0},{5,1},{6,2},{7,3},{8,12},{9,13},{10,... | collective-permute-start | bytes 2162696 | tf_op jit(solution)/shard_map/ppermute | solution.py:19
  167.8 69.5 %collective-permute-start.17 = (bf16[704,512]{1,0:T(8,128)(2,1)}, bf16[704,512]{1,0:T(8,128)(2,1)}, u32[]{:S(2)}, u32[]{:S(2)}) collective-permute-start(bf16[704,512]{1,0:T(8,128)(2,1)} %collective-permute-done.13.refs_2_), channel_id=1, source_target_pairs={{0,4},{1,5},{2,6},{3,7},{4,0},{5,1},{6,2},{7,3},{8,12},{9,13},{10,... | collective-permute-start | bytes 2162696 | tf_op jit(solution)/shard_map/ppermute | solution.py:19
  169.3 80.8 %collective-permute-start.18 = (bf16[704,512]{1,0:T(8,128)(2,1)}, bf16[704,512]{1,0:T(8,128)(2,1)}, u32[]{:S(2)}, u32[]{:S(2)}) collective-permute-start(bf16[704,512]{1,0:T(8,128)(2,1)} %collective-permute-done.14.refs_3_), channel_id=1, source_target_pairs={{0,4},{1,5},{2,6},{3,7},{4,0},{5,1},{6,2},{7,3},{8,12},{9,13},{10,... | collective-permute-start | bytes 2162696 | tf_op jit(solution)/shard_map/ppermute | solution.py:19
  326.4 75.9 %collective-permute-start.11 = (bf16[2,704,768]{2,1,0:T(8,128)(2,1)}, bf16[2,704,768]{2,1,0:T(8,128)(2,1)}, u32[]{:S(2)}, u32[]{:S(2)}) collective-permute-start(bf16[2,704,768]{2,1,0:T(8,128)(2,1)} %maximum_bitcast_fusion), channel_id=1, source_target_pairs={{0,1},{1,0},{2,3},{3,2},{4,5},{5,4},{6,7},{7,6},{8,9},{9,8},{10,11... | collective-permute-start | bytes 6488072 | tf_op jit(solution)/shard_map/ppermute | solution.py:19
  342.3 80.4 %collective-permute-start.32 = (bf16[704,768]{1,0:T(8,128)(2,1)S(1)}, bf16[704,768]{1,0:T(8,128)(2,1)}, u32[]{:S(2)}, u32[]{:S(2)}) collective-permute-start(bf16[704,768]{1,0:T(8,128)(2,1)S(1)} %fusion.1.refs_2_), channel_id=1, source_target_pairs={{0,8},{1,9},{2,10},{3,11},{4,12},{5,13},{6,14},{7,15},{8,16},{9,17... | collective-permute-start | bytes 3244040 | tf_op jit(solution)/shard_map/ppermute | solution.py:19
  385.6 138.7 %collective-permute-start.36 = (bf16[704,768]{1,0:T(8,128)(2,1)S(1)}, bf16[704,768]{1,0:T(8,128)(2,1)S(1)}, u32[]{:S(2)}, u32[]{:S(2)}) collective-permute-start(bf16[704,768]{1,0:T(8,128)(2,1)S(1)} %fusion.1.refs_2_), channel_id=1, source_target_pairs={{0,4},{1,5},{2,6},{3,7},{4,0},{5,1},{6,2},{7,3},{8,12},{9,13},{10,... | collective-permute-start | bytes 3244040 | tf_op jit(solution)/shard_map/ppermute | solution.py:19
  386.1 138.7 %collective-permute-start.28 = (bf16[704,768]{1,0:T(8,128)(2,1)S(1)}, bf16[704,768]{1,0:T(8,128)(2,1)}, u32[]{:S(2)}, u32[]{:S(2)}) collective-permute-start(bf16[704,768]{1,0:T(8,128)(2,1)S(1)} %fusion.1.refs_2_), channel_id=1, source_target_pairs={{0,16},{1,17},{2,18},{3,19},{4,20},{5,21},{6,22},{7,23},{8,24},{9,... | collective-permute-start | bytes 3244040 | tf_op jit(solution)/shard_map/ppermute | solution.py:19
  402.3 78.0 %collective-permute-start.29 = (bf16[704,512]{1,0:T(8,128)(2,1)}, bf16[704,512]{1,0:T(8,128)(2,1)S(1)}, u32[]{:S(2)}, u32[]{:S(2)}) collective-permute-start(bf16[704,512]{1,0:T(8,128)(2,1)} %fusion.3.refs_3_), channel_id=1, source_target_pairs={{0,16},{1,17},{2,18},{3,19},{4,20},{5,21},{6,22},{7,23},{8,24},{9,... | collective-permute-start | bytes 2162696 | tf_op jit(solution)/shard_map/ppermute | solution.py:19
  419.4 127.6 %collective-permute-start.24 = (bf16[704,768]{1,0:T(8,128)(2,1)S(1)}, bf16[704,768]{1,0:T(8,128)(2,1)S(1)}, u32[]{:S(2)}, u32[]{:S(2)}) collective-permute-start(bf16[704,768]{1,0:T(8,128)(2,1)S(1)} %fusion.1.refs_2_), channel_id=1, source_target_pairs={{0,24},{1,25},{2,26},{3,27},{4,28},{5,29},{6,30},{7,31},{8,0},{9,1... | collective-permute-start | bytes 3244040 | tf_op jit(solution)/shard_map/ppermute | solution.py:19
  422.8 125.2 %collective-permute-start.34 = (bf16[704,768]{1,0:T(8,128)(2,1)}, bf16[704,768]{1,0:T(8,128)(2,1)S(1)}, u32[]{:S(2)}, u32[]{:S(2)}) collective-permute-start(bf16[704,768]{1,0:T(8,128)(2,1)} %collective-permute-done.32.refs_2_), channel_id=1, source_target_pairs={{0,4},{1,5},{2,6},{3,7},{4,0},{5,1},{6,2},{7,3},{8,12},{9,13},{10,... | collective-permute-start | bytes 3244040 | tf_op jit(solution)/shard_map/ppermute | solution.py:19
  480.4 64.6 %collective-permute-start.25 = (bf16[704,512]{1,0:T(8,128)(2,1)}, bf16[704,512]{1,0:T(8,128)(2,1)}, u32[]{:S(2)}, u32[]{:S(2)}) collective-permute-start(bf16[704,512]{1,0:T(8,128)(2,1)} %fusion.3.refs_3_), channel_id=1, source_target_pairs={{0,24},{1,25},{2,26},{3,27},{4,28},{5,29},{6,30},{7,31},{8,0},{9,1... | collective-permute-start | bytes 2162696 | tf_op jit(solution)/shard_map/ppermute | solution.py:19
  525.3 57.0 %collective-permute-start.30 = (bf16[704,768]{1,0:T(8,128)(2,1)}, bf16[704,768]{1,0:T(8,128)(2,1)}, u32[]{:S(2)}, u32[]{:S(2)}) collective-permute-start(bf16[704,768]{1,0:T(8,128)(2,1)} %collective-permute-done.28.refs_2_), channel_id=1, source_target_pairs={{0,4},{1,5},{2,6},{3,7},{4,0},{5,1},{6,2},{7,3},{8,12},{9,13},{10,... | collective-permute-start | bytes 3244040 | tf_op jit(solution)/shard_map/ppermute | solution.py:19
  545.9 55.0 %collective-permute-start.27 = (bf16[704,512]{1,0:T(8,128)(2,1)}, bf16[704,512]{1,0:T(8,128)(2,1)}, u32[]{:S(2)}, u32[]{:S(2)}) collective-permute-start(bf16[704,512]{1,0:T(8,128)(2,1)} %collective-permute-done.25.refs_3_), channel_id=1, source_target_pairs={{0,4},{1,5},{2,6},{3,7},{4,0},{5,1},{6,2},{7,3},{8,12},{9,13},{10,... | collective-permute-start | bytes 2162696 | tf_op jit(solution)/shard_map/ppermute | solution.py:19
  547.0 71.9 %collective-permute-start.26 = (bf16[704,768]{1,0:T(8,128)(2,1)S(1)}, bf16[704,768]{1,0:T(8,128)(2,1)S(1)}, u32[]{:S(2)}, u32[]{:S(2)}) collective-permute-start(bf16[704,768]{1,0:T(8,128)(2,1)S(1)} %collective-permute-done.24.refs_2_), channel_id=1, source_target_pairs={{0,4},{1,5},{2,6},{3,7},{4,0},{5,1},{6,2},{7,3},{8,12},{9,13},{10,... | collective-permute-start | bytes 3244040 | tf_op jit(solution)/shard_map/ppermute | solution.py:19
  (30 other events, 1088.7 us)
where the time goes:
time: 640 us; the launch traced here: 638 us
  waiting for transfers between devices  331 us (52%)
  Pallas kernels  146 us (23%)
  starting transfers between devices  132 us (21%)
  other arithmetic  17.3 us (3%)
  local copies, waits for them, and re-layouts  12.5 us (2%)
    ppermute x38, waiting for transfers between devices, send(): lax.ppermute(value, 'tri', [(source, target(source)) for source in range(...  331 us
    ppermute x38, starting transfers between devices, send(): lax.ppermute(value, 'tri', [(source, target(source)) for source in range(...  132 us
    pallas_call x4, Pallas kernels, update(): pl.pallas_call(functools.partial(update_kernel, rows, units, parts, chain...  74.5 us
    pallas_call x4, Pallas kernels, image_terms(): pl.pallas_call(functools.partial(terms_kernel, rows, steps), out_shape=(o...  71.1 us
  transfers between devices with their start and end apart: 38, of which 13 were waited for; matrix products, arithmetic and copies ran while one was open for 4% of the time, Pallas kernels for 20%

commit v1 on v0

v1 whole, which is shorter than its diff:
```python
import functools

import jax
import jax.numpy as jnp
from jax import lax
from jax.experimental import pallas as pl
from jax.experimental.pallas import tpu as pltpu
from jax.sharding import PartitionSpec as P


STRIPES = 8
SIDES = 2
PLACES = STRIPES // SIDES
TOP, LOW, TURN = STRIPES, STRIPES + 1, STRIPES + 2
VMEM = 60 * 2**20


def send(value, target):
    count = lax.axis_size("tri")
    pairs = [(source, target(source)) for source in range(count)]
    return lax.ppermute(value, "tri", [pair for pair in pairs if pair[1] is not None])


def position(stripe):
    place, side = stripe // SIDES, stripe % SIDES
    return place + side * (STRIPES - 1 - 2 * place)


def stripe_at(position):
    up = position < PLACES
    return up * (SIDES * position) + (1 - up) * (2 * STRIPES - 1 - SIDES * position)


def ring_gather(own, band_size, forward):
    def hop(step):
        def target(source):
            stripe, column = source // band_size, source % band_size
            return stripe_at((position(stripe) + step) % STRIPES) * band_size + column

        return target

    pieces = {0: own}
    for step, hops in ((1, STRIPES // 2 - 1 + forward), (-1, STRIPES // 2 - forward)):
        held = own
        for count in range(1, hops + 1):
            held = send(held, hop(step))
            pieces[-step * count % STRIPES] = held
    return [pieces[distance] for distance in range(STRIPES)]


def across_gather(own, band_size):
    def target(source):
        stripe, column = source // band_size, source % band_size
        if stripe // SIDES in (0, PLACES - 1):
            return None
        return (stripe ^ 1) * band_size + column

    return send(own, target)


def row_block(rows):
    block = rows
    while block > 352 and block % 32 == 0:
        block //= 2
    return block


def fill_all(held, chunks, spans, where_ref, rows, sems):
    copies = []
    for index, (pieces, (start, end)) in enumerate(zip(chunks, spans)):
        for distance, piece in enumerate(pieces):
            at = pl.multiple_of(where_ref[distance] * rows, 16)
            into = held.at[pl.ds(at, rows), pl.ds(start, end - start)]
            copy = pltpu.make_async_copy(piece, into, sems.at[index, distance])
            copy.start()
            copies.append(copy)
    for copy in copies:
        copy.wait()


def terms_kernel(rows, steps, spans, where_ref, tile_ref, *refs):
    chunks = [refs[index * STRIPES : (index + 1) * STRIPES] for index in range(len(spans))]
    sent_ref, kept_ref, held, sems = refs[len(spans) * STRIPES :]
    step = pl.program_id(0)

    @pl.when(step == 0)
    def _():
        fill_all(held, chunks, spans, where_ref, rows, sems)

    product = jnp.dot(tile_ref[0], held[...], preferred_element_type=jnp.float32)
    product = product.astype(sent_ref.dtype)

    @pl.when(step < steps)
    def _():
        sent_ref[0] = product

    @pl.when(step >= steps)
    def _():
        kept_ref[0] = product


def image_terms(amplitudes, chunks, where, half, band_size):
    rows = chunks[0][0].shape[0]
    spans = chunk_spans([pieces[0].shape[1] for pieces in chunks])
    width = spans[-1][1]
    columns = amplitudes.shape[2]
    block = row_block(rows)
    parts = rows // block
    pairs = band_size // 4
    steps = pairs * parts

    def tile_index(step, where_ref):
        top, low = where_ref[TOP], where_ref[LOW]
        top = top if half else 1 - top
        second = step // steps
        place = step % steps // parts * 2 + jnp.where(second == 0, 1 - low, low)
        return 0, (top * pairs * 2 + place) * parts + step % parts, 0

    def sent_index(step, where_ref):
        at = jnp.minimum(step, steps - 1)
        return at // parts, at % parts, 0

    def kept_index(step, where_ref):
        at = jnp.maximum(step - steps, 0)
        return at // parts, at % parts, 0

    pieces = [piece for chunk in chunks for piece in chunk]
    out = jax.ShapeDtypeStruct((pairs, rows, width), jnp.bfloat16)
    return pl.pallas_call(
        functools.partial(terms_kernel, rows, steps, spans),
        out_shape=(out, out),
        grid_spec=pltpu.PrefetchScalarGridSpec(
            num_scalar_prefetch=1,
            grid=(2 * steps,),
            in_specs=[pl.BlockSpec((1, block, columns), tile_index)]
            + [pl.BlockSpec(memory_space=pl.ANY)] * len(pieces),
            out_specs=(
                pl.BlockSpec((1, block, width), sent_index),
                pl.BlockSpec((1, block, width), kept_index),
            ),
            scratch_shapes=[
                pltpu.VMEM((columns, width), jnp.bfloat16),
                pltpu.SemaphoreType.DMA((len(chunks), STRIPES)),
            ],
        ),
        compiler_params=pltpu.CompilerParams(vmem_limit_bytes=VMEM),
        cost_estimate=pl.CostEstimate(
            flops=4 * steps * block * columns * width,
            bytes_accessed=4 * steps * block * columns,
            transcendentals=0,
        ),
    )(where, amplitudes, *pieces)


def half_reduce(sent, kept, device, levels):
    received = send(sent, lambda source: source ^ 1)
    buffer = kept.astype(jnp.float32) + received.astype(jnp.float32)
    for level in range(1, levels):
        pairs = buffer.reshape(-1, 2, *buffer.shape[1:])
        bit = device // 2**level % 2
        keeping = lax.dynamic_index_in_dim(pairs, bit, 1, keepdims=False)
        outgoing = lax.dynamic_index_in_dim(pairs, 1 - bit, 1, keepdims=False)
        received = send(outgoing.astype(jnp.bfloat16), lambda source: source ^ 2**level)
        buffer = keeping + received.astype(jnp.float32)
    return buffer[0]


def band_gather(own, levels):
    blocks = {0: own}
    for level in reversed(range(levels)):
        for bits in list(blocks):
            other = bits ^ 2**level
            blocks[other] = send(blocks[bits], lambda source: source ^ 2**level)
    return [blocks[bits] for bits in range(2**levels)]


def band_kernel(spans, column_ref, *refs):
    pieces, (band_ref, sems) = refs[:-2], refs[-2:]
    count = len(pieces) // len(spans)
    rows = pieces[0].shape[0]
    copies = []
    for index, (start, end) in enumerate(spans):
        for bits in range(count):
            at = pl.multiple_of((column_ref[0] ^ bits) * rows, 16)
            into = band_ref.at[pl.ds(at, rows), pl.ds(start, end - start)]
            copy = pltpu.make_async_copy(pieces[index * count + bits], into, sems.at[index, bits])
            copy.start()
            copies.append(copy)
    for copy in copies:
        copy.wait()


def join_band(blocks, column):
    spans = chunk_spans([part[0].shape[1] for part in blocks])
    count, rows = len(blocks[0]), blocks[0][0].shape[0]
    shape = (count * rows, spans[-1][1])
    pieces = [block for part in blocks for block in part]
    return pl.pallas_call(
        functools.partial(band_kernel, spans),
        out_shape=jax.ShapeDtypeStruct(shape, jnp.bfloat16),
        grid_spec=pltpu.PrefetchScalarGridSpec(
            num_scalar_prefetch=1,
            grid=(1,),
            in_specs=[pl.BlockSpec(memory_space=pl.ANY)] * len(pieces),
            out_specs=pl.BlockSpec(shape, lambda step, column_ref: (0, 0)),
            scratch_shapes=[pltpu.SemaphoreType.DMA((len(spans), count))],
        ),
        compiler_params=pltpu.CompilerParams(vmem_limit_bytes=VMEM),
        cost_estimate=pl.CostEstimate(
            flops=2**30, bytes_accessed=4 * shape[0] * shape[1], transcendentals=0
        ),
    )(column.astype(jnp.int32)[None], *pieces)


def update_kernel(rows, turn, spans, keys, chained, where_ref, band_ref, *refs):
    chunks = []
    for names in keys:
        chunks.append(refs[: len(names)])
        refs = refs[len(names) :]
    row_ref, column_ref = refs[:2]
    out_ref, held, sems = refs[2 + chained :]

    @pl.when(pl.program_id(0) == 0)
    def _():
        if turn is None:
            fill_all(held, chunks, spans, where_ref, rows, sems)
            return
        waits = []
        for index, (pieces, names, (start, end)) in enumerate(zip(chunks, keys, spans)):
            for side in range(SIDES):
                distance = where_ref[TURN + 3 * turn + 1 + side]
                into = held.at[pl.ds(side * rows, rows), pl.ds(start, end - start)]
                for piece, name in zip(pieces, names):
                    copy = pltpu.make_async_copy(piece, into, sems.at[index, side])
                    wanted = distance == name[0]
                    for other in name[1:]:
                        wanted = wanted | (distance == other)
                    pl.when(wanted)(copy.start)
                waits.append(copy)
        for copy in waits:
            copy.wait()

    inner = lax.dot_general(
        band_ref[...], held[...], (((1,), (1,)), ((), ())), preferred_element_type=jnp.float32
    )
    out_ref[0] = -inner / (row_ref[...] + column_ref[0])


def update(band, chunks, keys, row_energy, column_energy, where, turn, earlier):
    rows = chunks[0][0].shape[0]
    height, depth = band.shape
    columns = STRIPES * rows
    span = columns if turn is None else SIDES * rows
    block = rows
    spans = chunk_spans([pieces[0].shape[1] for pieces in chunks])

    def at(where_ref):
        return 0 if turn is None else where_ref[TURN + 3 * turn]

    chained = int(earlier is not None)
    held = [piece for pieces in chunks for piece in pieces]
    in_specs = [pl.BlockSpec((block, depth), lambda step, where_ref: (step, 0))]
    in_specs += [pl.BlockSpec(memory_space=pl.ANY)] * len(held)
    in_specs += [
        pl.BlockSpec((block, 1), lambda step, where_ref: (step, 0)),
        pl.BlockSpec((1, 1, span), lambda step, where_ref: (at(where_ref), 0, 0)),
    ]
    operands = [where, band, *held, row_energy, column_energy.reshape(-1, 1, span)]
    aliases = {}
    if chained:
        aliases = {len(operands): 0}
        in_specs.append(pl.BlockSpec(memory_space=pl.ANY))
        operands.append(earlier)
    return pl.pallas_call(
        functools.partial(update_kernel, rows, turn, spans, keys, chained),
        out_shape=jax.ShapeDtypeStruct((1, height, columns), jnp.float32),
        grid_spec=pltpu.PrefetchScalarGridSpec(
            num_scalar_prefetch=1,
            grid=(height // block,),
            in_specs=in_specs,
            out_specs=pl.BlockSpec((1, block, span), lambda step, where_ref: (0, step, at(where_ref))),
            scratch_shapes=[
                pltpu.VMEM((span, depth), jnp.bfloat16),
                pltpu.SemaphoreType.DMA((len(chunks), STRIPES)),
            ],
        ),
        input_output_aliases=aliases,
        compiler_params=pltpu.CompilerParams(vmem_limit_bytes=VMEM),
        cost_estimate=pl.CostEstimate(
            flops=2 * height * span * depth,
            bytes_accessed=4 * height * span,
            transcendentals=0,
        ),
    )(*operands)


def chunk_spans(widths):
    spans, start = [], 0
    for width in widths:
        spans.append((start, start + width))
        start += width
    return spans


def split(width):
    first = -(-width // 256) * 128
    return [(0, first), (first, width)]


def per_device(amplitudes, factors, occ_energy, virt_energy):
    device = lax.axis_index("tri")
    band_size = lax.axis_size("tri") // STRIPES
    levels = band_size.bit_length() - 1
    rows, naux = factors.shape
    stripe, column = device // band_size, device % band_size
    pair_energy = (virt_energy[None, :] - occ_energy[:, None]).reshape(-1)
    grid = pair_energy.reshape(STRIPES, band_size, rows)
    row_energy = lax.dynamic_index_in_dim(grid, stripe, 0, keepdims=False).reshape(-1)
    column_energy = lax.dynamic_index_in_dim(grid, column, 1, keepdims=False).reshape(-1)
    place = stripe // SIDES
    here = position(stripe)
    table = [stripe_at((here + distance) % STRIPES) for distance in range(STRIPES)]
    table += [column // (band_size // 2), column % 2]
    for turn in range(PLACES):
        unit = place ^ turn
        table.append(unit)
        table += [(position(unit * SIDES + side) - here) % STRIPES for side in range(SIDES)]
    where = jnp.stack([jnp.asarray(entry, jnp.int32) for entry in table])

    first = naux // 512 * 256
    bands, gathered, beside = [], [], []
    for part, own in enumerate((factors[:, :first], factors[:, first:])):
        cuts = split(own.shape[1])
        chunks = [
            ring_gather(own[:, start:end], band_size, index == part % 2)
            for index, (start, end) in enumerate(cuts)
        ]
        halves = []
        for half in range(2):
            sent, kept = image_terms(amplitudes, chunks, where, half, band_size)
            halves.append(half_reduce(sent, kept, device, levels - 1))
        received = send(halves[0].astype(jnp.bfloat16), lambda source: source ^ band_size // 2)
        images = halves[1] + received.astype(jnp.float32) + own.astype(jnp.float32)
        dressed = images.astype(jnp.bfloat16)
        for index, (start, end) in enumerate(cuts):
            chunk = dressed[:, start:end]
            gathered.append(ring_gather(chunk, band_size, index == part % 2))
            beside.append(across_gather(chunk, band_size))
        bands.append(band_gather(dressed, levels))
    band = join_band(bands, column)

    row_energy = row_energy[:, None]
    energies = (row_energy, column_energy, where)
    whole = tuple((distance,) for distance in range(STRIPES))
    if rows * SIDES % 128:
        return update(band, gathered, [whole] * len(gathered), *energies, None, None)
    result = None
    for turn in range(PLACES):
        chunks, keys = [], []
        for pieces, other in zip(gathered, beside):
            reach = [d for d in range(STRIPES) if min(d, STRIPES - d) <= turn + 1]
            chunk = [pieces[d] for d in reach]
            names = [(d,) for d in reach]
            if turn == 0:
                chunk.append(other)
                names.append((3, 5))
            chunks.append(chunk)
            keys.append(tuple(names))
        result = update(band, chunks, keys, *energies, turn, result)
    return result


def solution(mesh):
    placed = (P("tri", None, None), P("tri", None), P(), P())
    return jax.shard_map(
        per_device, mesh=mesh, in_specs=placed, out_specs=P("tri", None, None), check_vma=False
    )
```

time: 640 us -> 400 us (0.62)
  waiting for transfers between devices: 331 us -> 135 us
  starting transfers between devices: 132 us -> 92.3 us
  other arithmetic: 17.3 us -> 2.29 us
  Pallas kernels: 146 us -> 155 us
    ppermute x38 -> x72, waiting for transfers between devices: 331 us -> 135 us  [send(): lax.ppermute(value, 'tri', [pair for pair in pairs if pair[1] is not None])]
    ppermute x38 -> x72, starting transfers between devices: 132 us -> 92.3 us  [send(): lax.ppermute(value, 'tri', [pair for pair in pairs if pair[1] is not None])]
    pallas_call x8 -> x9, Pallas kernels: 146 us -> 155 us  [the longest x4 74.6 us: image_terms(): pl.pallas_call(functools.partial(terms_kernel, rows, steps, spans), out_s...]
    another operation x7 -> x0, other arithmetic: 7.86 us -> none  [the longest x6 7.31 us: band_gather(): buffer = jnp.stack([first, second], 1).reshape(-1, rows, width)]
  transfers between devices with their start and end apart: 38 -> 72, of which waited for: 13 -> 31; matrix products, arithmetic and copies ran while one was open for 4% -> 2% of each run, Pallas kernels for 20% -> 34%
where the time goes in v1:
time: 400 us; the launch traced here: 399 us
  Pallas kernels  155 us (39%)
  waiting for transfers between devices  135 us (34%)
  starting transfers between devices  92.3 us (23%)
  local copies, waits for them, and re-layouts  13 us (3%)
    ppermute x72, waiting for transfers between devices, send(): lax.ppermute(value, 'tri', [pair for pair in pairs if pair[1] is not None])  135 us
    ppermute x72, starting transfers between devices, send(): lax.ppermute(value, 'tri', [pair for pair in pairs if pair[1] is not None])  92.3 us
    pallas_call x4, Pallas kernels, image_terms(): pl.pallas_call(functools.partial(terms_kernel, rows, steps, spans), out_s...  74.6 us
    pallas_call x4, Pallas kernels, update(): pl.pallas_call(functools.partial(update_kernel, rows, turn, spans, keys,...  74.6 us
  transfers between devices with their start and end apart: 72, of which 31 were waited for; matrix products, arithmetic and copies ran while one was open for 2% of the time, Pallas kernels for 34%

profile of v1, /device:TPU:0, one launch (start us, length us, event | category | flops | bytes accessed | tf_op | source)
XLA Modules:
  0.0 399.4 jit_solution(4176178414469746276)
XLA Ops:
  17.1 15.7 %collective-permute-done.3.refs_7_ = bf16[704,256]{1,0:T(8,128)(2,1)S(1)} collective-permute-done((bf16[704,256]{1,0:T(8,128)(2,1)S(1)}, bf16[704,256]{1,0:T(8,128)(2,1)S(1)}, u32[]{:S(2)}, u32[]{:S(2)}) %collective-permute-start.3) | collective-permute-done | bytes 360480 | tf_op jit(solution)/shard_map/ppermute | solution.py:21
  37.1 7.4 %collective-permute-done.24.refs_7_ = bf16[704,384]{1,0:T(8,128)(2,1)} collective-permute-done((bf16[704,384]{1,0:T(8,128)(2,1)S(1)}, bf16[704,384]{1,0:T(8,128)(2,1)}, u32[]{:S(2)}, u32[]{:S(2)}) %collective-permute-start.24) | collective-permute-done | bytes 540704 | tf_op jit(solution)/shard_map/ppermute | solution.py:21
  46.5 5.6 %collective-permute-done.12.refs_14_ = bf16[704,256]{1,0:T(8,128)(2,1)S(1)} collective-permute-done((bf16[704,256]{1,0:T(8,128)(2,1)S(1)}, bf16[704,256]{1,0:T(8,128)(2,1)S(1)}, u32[]{:S(2)}, u32[]{:S(2)}) %collective-permute-start.12) | collective-permute-done | bytes 360480 | tf_op jit(solution)/shard_map/ppermute | solution.py:21
  80.9 6.0 %collective-permute-done.31.refs_14_ = bf16[704,384]{1,0:T(8,128)(2,1)S(1)} collective-permute-done((bf16[704,384]{1,0:T(8,128)(2,1)S(1)}, bf16[704,384]{1,0:T(8,128)(2,1)S(1)}, u32[]{:S(2)}, u32[]{:S(2)}) %collective-permute-start.31) | collective-permute-done | bytes 540704 | tf_op jit(solution)/shard_map/ppermute | solution.py:21
  92.6 5.9 %collective-permute-done.25.refs_6_ = bf16[704,384]{1,0:T(8,128)(2,1)} collective-permute-done((bf16[704,384]{1,0:T(8,128)(2,1)}, bf16[704,384]{1,0:T(8,128)(2,1)}, u32[]{:S(2)}, u32[]{:S(2)}) %collective-permute-start.25) | collective-permute-done | bytes 540704 | tf_op jit(solution)/shard_map/ppermute | solution.py:21
  104.2 5.7 %collective-permute-done.10.refs_12_ = bf16[704,256]{1,0:T(8,128)(2,1)} collective-permute-done((bf16[704,256]{1,0:T(8,128)(2,1)}, bf16[704,256]{1,0:T(8,128)(2,1)}, u32[]{:S(2)}, u32[]{:S(2)}) %collective-permute-start.10) | collective-permute-done | bytes 360480 | tf_op jit(solution)/shard_map/ppermute | solution.py:21
  111.9 16.1 %shard_map.47 = (bf16[1,704,512]{2,1,0:T(8,128)(2,1)}, bf16[1,704,512]{2,1,0:T(8,128)(2,1)}) custom-call(s32[22]{0:T(128)} %stack.91.where_ref, bf16[1,2816,5632]{2,1,0:T(8,128)(2,1)} %tile_ref.7, bf16[704,256]{1,0:T(8,128)(2,1)} %copy-done.21, bf16[704,256]{1,0:T(8,128)(2,1)} %copy-done.28, bf16[704,256]{1,0:T(8,128)(2,1)} %copy-done.32, ...), custom_call_target="tpu_custom_call" | custom-call | flops 8120172544 | bytes 15859712 | tf_op jit(solution)/shard_map/pallas_call | solution.py:129
  131.9 16.0 %shard_map.46 = (bf16[1,704,512]{2,1,0:T(8,128)(2,1)}, bf16[1,704,512]{2,1,0:T(8,128)(2,1)}) custom-call(s32[22]{0:T(128)} %stack.91.where_ref, bf16[1,2816,5632]{2,1,0:T(8,128)(2,1)} %tile_ref.7, bf16[704,256]{1,0:T(8,128)(2,1)} %copy-done.21, bf16[704,256]{1,0:T(8,128)(2,1)} %copy-done.28, bf16[704,256]{1,0:T(8,128)(2,1)} %copy-done.32, ...), custom_call_target="tpu_custom_call" | custom-call | flops 8120172544 | bytes 15859712 | tf_op jit(solution)/shard_map/pallas_call | solution.py:129
  151.4 21.2 %shard_map.49 = (bf16[1,704,768]{2,1,0:T(8,128)(2,1)}, bf16[1,704,768]{2,1,0:T(8,128)(2,1)}) custom-call(s32[22]{0:T(128)} %stack.91.where_ref, bf16[1,2816,5632]{2,1,0:T(8,128)(2,1)} %tile_ref.7, bf16[704,384]{1,0:T(8,128)(2,1)} %copy-done.50, bf16[704,384]{1,0:T(8,128)(2,1)} %collective-permute-done.20.refs_1_, ...), custom_call_target="tpu_custom_call" | custom-call | flops 12180258816 | bytes 15859712 | tf_op jit(solution)/shard_map/pallas_call | solution.py:129
  172.8 21.3 %shard_map.48 = (bf16[1,704,768]{2,1,0:T(8,128)(2,1)}, bf16[1,704,768]{2,1,0:T(8,128)(2,1)}) custom-call(s32[22]{0:T(128)} %stack.91.where_ref, bf16[1,2816,5632]{2,1,0:T(8,128)(2,1)} %tile_ref.7, bf16[704,384]{1,0:T(8,128)(2,1)} %copy-done.50, bf16[704,384]{1,0:T(8,128)(2,1)} %collective-permute-done.20.refs_1_, ...), custom_call_target="tpu_custom_call" | custom-call | flops 12180258816 | bytes 15859712 | tf_op jit(solution)/shard_map/pallas_call | solution.py:129
  197.3 4.4 %collective-permute-start.51 = (bf16[704,256]{1,0:T(8,128)(2,1)S(1)}, bf16[704,256]{1,0:T(8,128)(2,1)S(1)}, u32[]{:S(2)}, u32[]{:S(2)}) collective-permute-start(bf16[704,256]{1,0:T(8,128)(2,1)S(1)} %get-tuple-element.27.refs_4_.refs_5_.refs_7_.refs_8_), channel_id=1, source_target_pairs={{0,8},{1,9},{2,10},{3,11},{4,0},{5,1},{6,2},{7,3},{8,16},{9,17},{1... | collective-permute-start | bytes 1081352 | tf_op jit(solution)/shard_map/ppermute | solution.py:21
  201.8 19.1 %collective-permute-done.36 = bf16[704,768]{1,0:T(8,128)(2,1)S(1)} collective-permute-done((bf16[704,768]{1,0:T(8,128)(2,1)S(1)}, bf16[704,768]{1,0:T(8,128)(2,1)S(1)}, u32[]{:S(2)}, u32[]{:S(2)}) %collective-permute-start.36) | collective-permute-done | bytes 1081376 | tf_op jit(solution)/shard_map/ppermute | solution.py:21
  224.3 4.4 %collective-permute-start.43 = (bf16[704,256]{1,0:T(8,128)(2,1)S(1)}, bf16[704,256]{1,0:T(8,128)(2,1)S(1)}, u32[]{:S(2)}, u32[]{:S(2)}) collective-permute-start(bf16[704,256]{1,0:T(8,128)(2,1)S(1)} %get-tuple-element.28.refs_0_), channel_id=1, source_target_pairs={{0,8},{1,9},{2,10},{3,11},{4,0},{5,1},{6,2},{7,3},{8,16},{9,17},{1... | collective-permute-start | bytes 1081352 | tf_op jit(solution)/shard_map/ppermute | solution.py:21
  228.8 4.5 %collective-permute-done.47.refs_5_.refs_6_.refs_8_.refs_9_ = bf16[704,256]{1,0:T(8,128)(2,1)S(1)} collective-permute-done((bf16[704,256]{1,0:T(8,128)(2,1)S(1)}, bf16[704,256]{1,0:T(8,128)(2,1)S(1)}, u32[]{:S(2)}, u32[]{:S(2)}) %collective-permute-start.47) | collective-permute-done | bytes 360480 | tf_op jit(solution)/shard_map/ppermute | solution.py:21
  251.2 5.7 %collective-permute-done.41.refs_2_ = bf16[704,256]{1,0:T(8,128)(2,1)S(1)} collective-permute-done((bf16[704,256]{1,0:T(8,128)(2,1)S(1)}, bf16[704,256]{1,0:T(8,128)(2,1)S(1)}, u32[]{:S(2)}, u32[]{:S(2)}) %collective-permute-start.41) | collective-permute-done | bytes 360480 | tf_op jit(solution)/shard_map/ppermute | solution.py:21
  266.7 9.7 %collective-permute-done.49.refs_10_.refs_11_ = bf16[704,256]{1,0:T(8,128)(2,1)} collective-permute-done((bf16[704,256]{1,0:T(8,128)(2,1)S(1)}, bf16[704,256]{1,0:T(8,128)(2,1)}, u32[]{:S(2)}, u32[]{:S(2)}) %collective-permute-start.49) | collective-permute-done | bytes 360480 | tf_op jit(solution)/shard_map/ppermute | solution.py:21
  280.0 4.1 %collective-permute-start.58 = (bf16[704,384]{1,0:T(8,128)(2,1)S(1)}, bf16[704,384]{1,0:T(8,128)(2,1)}, u32[]{:S(2)}, u32[]{:S(2)}) collective-permute-start(bf16[704,384]{1,0:T(8,128)(2,1)S(1)} %get-tuple-element.26.refs_8_.refs_10_.refs_14_.refs_16_), channel_id=1, source_target_pairs={{0,8},{1,9},{2,10},{3,11},{4,0},{5,1},{6,2},{7,3},{8,16},{9,17},{1... | collective-permute-start | bytes 1622024 | tf_op jit(solution)/shard_map/ppermute | solution.py:21
  288.7 6.1 %shard_map.50.band_ref = bf16[2816,1280]{1,0:T(8,128)(2,1)} custom-call(s32[1]{0:T(128)} %bitcast.22.column_ref, bf16[704,512]{1,0:T(8,128)(2,1)} %copy-done.8, bf16[704,512]{1,0:T(8,128)(2,1)} %copy-done.44, bf16[704,512]{1,0:T(8,128)(2,1)} %copy-done.43, bf16[704,512]{1,0:T(8,128)(2,1)} %copy-done.45, bf16[704,768]{1,0:T(8,128)(2,1)} %copy-done.2, ...), custom_call_target="tpu_custom_call" | custom-call | flops 1073741824 | bytes 14417920 | tf_op jit(solution)/shard_map/pallas_call | solution.py:198
  299.0 4.4 %collective-permute-done.58.refs_10_.refs_14_.refs_20_.refs_23_ = bf16[704,384]{1,0:T(8,128)(2,1)} collective-permute-done((bf16[704,384]{1,0:T(8,128)(2,1)S(1)}, bf16[704,384]{1,0:T(8,128)(2,1)}, u32[]{:S(2)}, u32[]{:S(2)}) %collective-permute-start.58) | collective-permute-done | bytes 540704 | tf_op jit(solution)/shard_map/ppermute | solution.py:21
  305.4 18.6 %shard_map.51.refs_22_ = f32[1,2816,5632]{2,1,0:T(8,128)} custom-call(s32[22]{0:T(128)} %stack.91.where_ref, bf16[2816,1280]{1,0:T(8,128)(2,1)} %shard_map.50.band_ref, bf16[704,256]{1,0:T(8,128)(2,1)} %copy-done.4, bf16[704,256]{1,0:T(8,128)(2,1)} %copy-done.12, bf16[704,256]{1,0:T(8,128)(2,1)} %copy-done.11, bf16[704,256]{1,0:T(8,128)(2,1)} %copy-done.52, ...), custom_call_target="tpu_custom_call" | custom-call | flops 10150215680 | bytes 15859712 | tf_op jit(solution)/shard_map/pallas_call | solution.py:274
  326.2 7.9 %collective-permute-done.59.refs_13_.refs_19_.refs_22_ = bf16[704,384]{1,0:T(8,128)(2,1)S(1)} collective-permute-done((bf16[704,384]{1,0:T(8,128)(2,1)}, bf16[704,384]{1,0:T(8,128)(2,1)S(1)}, u32[]{:S(2)}, u32[]{:S(2)}) %collective-permute-start.59) | collective-permute-done | bytes 540704 | tf_op jit(solution)/shard_map/ppermute | solution.py:21
  336.7 18.6 %shard_map.52.refs_30_ = f32[1,2816,5632]{2,1,0:T(8,128)} custom-call(s32[22]{0:T(128)} %stack.91.where_ref, bf16[2816,1280]{1,0:T(8,128)(2,1)} %shard_map.50.band_ref, bf16[704,256]{1,0:T(8,128)(2,1)} %copy-done.4, bf16[704,256]{1,0:T(8,128)(2,1)} %copy-done.12, bf16[704,256]{1,0:T(8,128)(2,1)} %copy-done.19, ...), custom_call_target="tpu_custom_call", output_to_operand_aliasing={{}: (24, {})} | custom-call | flops 10150215680 | bytes 15859712 | tf_op jit(solution)/shard_map/pallas_call | solution.py:274
  360.2 18.6 %shard_map.53.refs_34_ = f32[1,2816,5632]{2,1,0:T(8,128)} custom-call(s32[22]{0:T(128)} %stack.91.where_ref, bf16[2816,1280]{1,0:T(8,128)(2,1)} %shard_map.50.band_ref, bf16[704,256]{1,0:T(8,128)(2,1)} %copy-done.4, bf16[704,256]{1,0:T(8,128)(2,1)} %copy-done.12, bf16[704,256]{1,0:T(8,128)(2,1)} %copy-done.19, ...), custom_call_target="tpu_custom_call", output_to_operand_aliasing={{}: (32, {})} | custom-call | flops 10150215680 | bytes 15859712 | tf_op jit(solution)/shard_map/pallas_call | solution.py:274
  380.5 18.6 %shard_map.54 = f32[1,2816,5632]{2,1,0:T(8,128)} custom-call(s32[22]{0:T(128)} %stack.91.where_ref, bf16[2816,1280]{1,0:T(8,128)(2,1)} %shard_map.50.band_ref, bf16[704,256]{1,0:T(8,128)(2,1)} %copy-done.4, bf16[704,256]{1,0:T(8,128)(2,1)} %copy-done.12, bf16[704,256]{1,0:T(8,128)(2,1)} %copy-done.19, ...), custom_call_target="tpu_custom_call", output_to_operand_aliasing={{}: (36, {})} | custom-call | flops 10150215680 | bytes 15859712 | tf_op jit(solution)/shard_map/pallas_call | solution.py:274
  (260 shorter events, 132.4 us)
Async XLA Ops:
  5.6 29.4 %collective-permute-start.30 = (bf16[704,384]{1,0:T(8,128)(2,1)S(1)}, bf16[704,384]{1,0:T(8,128)(2,1)S(1)}, u32[]{:S(2)}, u32[]{:S(2)}) collective-permute-start(bf16[704,384]{1,0:T(8,128)(2,1)S(1)} %get-tuple-element.21.refs_8_), channel_id=1, source_target_pairs={{0,8},{1,9},{2,10},{3,11},{4,0},{5,1},{6,2},{7,3},{8,16},{9,17},{1... | collective-permute-start | bytes 1622024 | tf_op jit(solution)/shard_map/ppermute | solution.py:21
  7.7 29.2 %collective-permute-start.27 = (bf16[704,384]{1,0:T(8,128)(2,1)S(1)}, bf16[704,384]{1,0:T(8,128)(2,1)}, u32[]{:S(2)}, u32[]{:S(2)}) collective-permute-start(bf16[704,384]{1,0:T(8,128)(2,1)S(1)} %get-tuple-element.21.refs_8_), channel_id=1, source_target_pairs={{0,4},{1,5},{2,6},{3,7},{4,12},{5,13},{6,14},{7,15},{8,0},{9,1},{1... | collective-permute-start | bytes 1622024 | tf_op jit(solution)/shard_map/ppermute | solution.py:21
  15.6 28.9 %collective-permute-start.24 = (bf16[704,384]{1,0:T(8,128)(2,1)S(1)}, bf16[704,384]{1,0:T(8,128)(2,1)}, u32[]{:S(2)}, u32[]{:S(2)}) collective-permute-start(bf16[704,384]{1,0:T(8,128)(2,1)S(1)} %get-tuple-element.22.refs_0_), channel_id=1, source_target_pairs={{0,8},{1,9},{2,10},{3,11},{4,0},{5,1},{6,2},{7,3},{8,16},{9,17},{1... | collective-permute-start | bytes 1622024 | tf_op jit(solution)/shard_map/ppermute | solution.py:21
  32.8 29.1 %collective-permute-start.20 = (bf16[704,384]{1,0:T(8,128)(2,1)S(1)}, bf16[704,384]{1,0:T(8,128)(2,1)}, u32[]{:S(2)}, u32[]{:S(2)}) collective-permute-start(bf16[704,384]{1,0:T(8,128)(2,1)S(1)} %get-tuple-element.22.refs_0_), channel_id=1, source_target_pairs={{0,4},{1,5},{2,6},{3,7},{4,12},{5,13},{6,14},{7,15},{8,0},{9,1},{1... | collective-permute-start | bytes 1622024 | tf_op jit(solution)/shard_map/ppermute | solution.py:21
  71.3 27.3 %collective-permute-start.25 = (bf16[704,384]{1,0:T(8,128)(2,1)}, bf16[704,384]{1,0:T(8,128)(2,1)}, u32[]{:S(2)}, u32[]{:S(2)}) collective-permute-start(bf16[704,384]{1,0:T(8,128)(2,1)} %collective-permute-done.24.refs_7_), channel_id=1, source_target_pairs={{0,8},{1,9},{2,10},{3,11},{4,0},{5,1},{6,2},{7,3},{8,16},{9,17},{1... | collective-permute-start | bytes 1622024 | tf_op jit(solution)/shard_map/ppermute | solution.py:21
  78.9 31.0 %collective-permute-start.10 = (bf16[704,256]{1,0:T(8,128)(2,1)}, bf16[704,256]{1,0:T(8,128)(2,1)}, u32[]{:S(2)}, u32[]{:S(2)}) collective-permute-start(bf16[704,256]{1,0:T(8,128)(2,1)} %collective-permute-done.9.refs_11_), channel_id=1, source_target_pairs={{0,4},{1,5},{2,6},{3,7},{4,12},{5,13},{6,14},{7,15},{8,0},{9,1},{1... | collective-permute-start | bytes 1081352 | tf_op jit(solution)/shard_map/ppermute | solution.py:21
  90.6 37.5 %collective-permute-start.32 = (bf16[704,384]{1,0:T(8,128)(2,1)}, bf16[704,384]{1,0:T(8,128)(2,1)}, u32[]{:S(2)}, u32[]{:S(2)}) collective-permute-start(bf16[704,384]{1,0:T(8,128)(2,1)} %copy-done.56), channel_id=1, source_target_pairs={{0,8},{1,9},{2,10},{3,11},{4,0},{5,1},{6,2},{7,3},{8,16},{9,17},{1... | collective-permute-start | bytes 1622024 | tf_op jit(solution)/shard_map/ppermute | solution.py:21
  98.6 50.5 %collective-permute-start.29 = (bf16[704,384]{1,0:T(8,128)(2,1)}, bf16[704,384]{1,0:T(8,128)(2,1)}, u32[]{:S(2)}, u32[]{:S(2)}) collective-permute-start(bf16[704,384]{1,0:T(8,128)(2,1)} %collective-permute-done.28.refs_10_), channel_id=1, source_target_pairs={{0,4},{1,5},{2,6},{3,7},{4,12},{5,13},{6,14},{7,15},{8,0},{9,1},{1... | collective-permute-start | bytes 1622024 | tf_op jit(solution)/shard_map/ppermute | solution.py:21
  102.2 48.4 %collective-permute-start.26 = (bf16[704,384]{1,0:T(8,128)(2,1)}, bf16[704,384]{1,0:T(8,128)(2,1)}, u32[]{:S(2)}, u32[]{:S(2)}) collective-permute-start(bf16[704,384]{1,0:T(8,128)(2,1)} %collective-permute-done.25.refs_6_), channel_id=1, source_target_pairs={{0,8},{1,9},{2,10},{3,11},{4,0},{5,1},{6,2},{7,3},{8,16},{9,17},{1... | collective-permute-start | bytes 1622024 | tf_op jit(solution)/shard_map/ppermute | solution.py:21
  148.0 47.3 %collective-permute-start.14 = (bf16[1,704,512]{2,1,0:T(8,128)(2,1)}, bf16[1,704,512]{2,1,0:T(8,128)(2,1)S(1)}, u32[]{:S(2)}, u32[]{:S(2)}) collective-permute-start(bf16[1,704,512]{2,1,0:T(8,128)(2,1)} %get-tuple-element.14), channel_id=1, source_target_pairs={{0,1},{1,0},{2,3},{3,2},{4,5},{5,4},{6,7},{7,6},{8,9},{9,8},{10,11... | collective-permute-start | bytes 2162696 | tf_op jit(solution)/shard_map/ppermute | solution.py:21
  149.1 46.2 %collective-permute-start.16 = (bf16[704,512]{1,0:T(8,128)(2,1)}, bf16[704,512]{1,0:T(8,128)(2,1)S(1)}, u32[]{:S(2)}, u32[]{:S(2)}) collective-permute-start(bf16[704,512]{1,0:T(8,128)(2,1)} %fusion.5), channel_id=1, source_target_pairs={{0,2},{1,3},{2,0},{3,1},{4,6},{5,7},{6,4},{7,5},{8,10},{9,11},{10,... | collective-permute-start | bytes 2162696 | tf_op jit(solution)/shard_map/ppermute | solution.py:21
  196.5 27.8 %collective-permute-start.69 = (bf16[704,256]{1,0:T(8,128)(2,1)S(1)}, bf16[704,256]{1,0:T(8,128)(2,1)S(1)}, u32[]{:S(2)}, u32[]{:S(2)}) collective-permute-start(bf16[704,256]{1,0:T(8,128)(2,1)S(1)} %get-tuple-element.27.refs_4_.refs_5_.refs_7_.refs_8_), channel_id=1, source_target_pairs={{8,12},{9,13},{10,14},{11,15},{12,8},{13,9},{14,10},{15,11},{16,20... | collective-permute-start | bytes 1081352 | tf_op jit(solution)/shard_map/ppermute | solution.py:21
  197.3 31.4 %collective-permute-start.51 = (bf16[704,256]{1,0:T(8,128)(2,1)S(1)}, bf16[704,256]{1,0:T(8,128)(2,1)S(1)}, u32[]{:S(2)}, u32[]{:S(2)}) collective-permute-start(bf16[704,256]{1,0:T(8,128)(2,1)S(1)} %get-tuple-element.27.refs_4_.refs_5_.refs_7_.refs_8_), channel_id=1, source_target_pairs={{0,8},{1,9},{2,10},{3,11},{4,0},{5,1},{6,2},{7,3},{8,16},{9,17},{1... | collective-permute-start | bytes 1081352 | tf_op jit(solution)/shard_map/ppermute | solution.py:21
  221.4 29.2 %collective-permute-start.38 = (bf16[704,768]{1,0:T(8,128)(2,1)S(1)}, bf16[704,768]{1,0:T(8,128)(2,1)S(1)}, u32[]{:S(2)}, u32[]{:S(2)}) collective-permute-start(bf16[704,768]{1,0:T(8,128)(2,1)S(1)} %fusion.1.refs_4_), channel_id=1, source_target_pairs={{0,2},{1,3},{2,0},{3,1},{4,6},{5,7},{6,4},{7,5},{8,10},{9,11},{10,... | collective-permute-start | bytes 3244040 | tf_op jit(solution)/shard_map/ppermute | solution.py:21
  250.7 29.4 %collective-permute-start.37 = (bf16[704,768]{1,0:T(8,128)(2,1)S(1)}, bf16[704,768]{1,0:T(8,128)(2,1)S(1)}, u32[]{:S(2)}, u32[]{:S(2)}) collective-permute-start(bf16[704,768]{1,0:T(8,128)(2,1)S(1)} %fusion.1.refs_4_), channel_id=1, source_target_pairs={{0,1},{1,0},{2,3},{3,2},{4,5},{5,4},{6,7},{7,6},{8,9},{9,8},{10,11... | collective-permute-start | bytes 3244040 | tf_op jit(solution)/shard_map/ppermute | solution.py:21
  250.7 33.5 %collective-permute-start.39 = (bf16[704,768]{1,0:T(8,128)(2,1)S(1)}, bf16[704,768]{1,0:T(8,128)(2,1)S(1)}, u32[]{:S(2)}, u32[]{:S(2)}) collective-permute-start(bf16[704,768]{1,0:T(8,128)(2,1)S(1)} %collective-permute-done.38.refs_6_), channel_id=1, source_target_pairs={{0,1},{1,0},{2,3},{3,2},{4,5},{5,4},{6,7},{7,6},{8,9},{9,8},{10,11... | collective-permute-start | bytes 3244040 | tf_op jit(solution)/shard_map/ppermute | solution.py:21
  294.9 29.2 %collective-permute-start.45 = (bf16[704,256]{1,0:T(8,128)(2,1)}, bf16[704,256]{1,0:T(8,128)(2,1)}, u32[]{:S(2)}, u32[]{:S(2)}) collective-permute-start(bf16[704,256]{1,0:T(8,128)(2,1)} %collective-permute-done.44.refs_3_.refs_5_.refs_6_), channel_id=1, source_target_pairs={{0,8},{1,9},{2,10},{3,11},{4,0},{5,1},{6,2},{7,3},{8,16},{9,17},{1... | collective-permute-start | bytes 1081352 | tf_op jit(solution)/shard_map/ppermute | solution.py:21
  296.9 27.2 %collective-permute-start.65 = (bf16[704,384]{1,0:T(8,128)(2,1)S(1)}, bf16[704,384]{1,0:T(8,128)(2,1)S(1)}, u32[]{:S(2)}, u32[]{:S(2)}) collective-permute-start(bf16[704,384]{1,0:T(8,128)(2,1)S(1)} %collective-permute-done.64.refs_14_.refs_19_.refs_27_.refs_31_), channel_id=1, source_target_pairs={{0,8},{1,9},{2,10},{3,11},{4,0},{5,1},{6,2},{7,3},{8,16},{9,17},{1... | collective-permute-start | bytes 1622024 | tf_op jit(solution)/shard_map/ppermute | solution.py:21
  298.5 27.6 %collective-permute-start.62 = (bf16[704,384]{1,0:T(8,128)(2,1)S(1)}, bf16[704,384]{1,0:T(8,128)(2,1)S(1)}, u32[]{:S(2)}, u32[]{:S(2)}) collective-permute-start(bf16[704,384]{1,0:T(8,128)(2,1)S(1)} %collective-permute-done.61.refs_13_.refs_16_.refs_22_.refs_25_), channel_id=1, source_target_pairs={{0,4},{1,5},{2,6},{3,7},{4,12},{5,13},{6,14},{7,15},{8,0},{9,1},{1... | collective-permute-start | bytes 1622024 | tf_op jit(solution)/shard_map/ppermute | solution.py:21
  303.3 30.8 %collective-permute-start.59 = (bf16[704,384]{1,0:T(8,128)(2,1)}, bf16[704,384]{1,0:T(8,128)(2,1)S(1)}, u32[]{:S(2)}, u32[]{:S(2)}) collective-permute-start(bf16[704,384]{1,0:T(8,128)(2,1)} %collective-permute-done.58.refs_10_.refs_14_.refs_20_.refs_23_), channel_id=1, source_target_pairs={{0,8},{1,9},{2,10},{3,11},{4,0},{5,1},{6,2},{7,3},{8,16},{9,17},{1... | collective-permute-start | bytes 1622024 | tf_op jit(solution)/shard_map/ppermute | solution.py:21
  305.1 30.8 %collective-permute-start.55 = (bf16[704,384]{1,0:T(8,128)(2,1)}, bf16[704,384]{1,0:T(8,128)(2,1)S(1)}, u32[]{:S(2)}, u32[]{:S(2)}) collective-permute-start(bf16[704,384]{1,0:T(8,128)(2,1)} %collective-permute-done.54.refs_9_.refs_11_.refs_15_.refs_17_), channel_id=1, source_target_pairs={{0,4},{1,5},{2,6},{3,7},{4,12},{5,13},{6,14},{7,15},{8,0},{9,1},{1... | collective-permute-start | bytes 1622024 | tf_op jit(solution)/shard_map/ppermute | solution.py:21
  324.0 31.3 %collective-permute-start.42 = (bf16[704,256]{1,0:T(8,128)(2,1)}, bf16[704,256]{1,0:T(8,128)(2,1)}, u32[]{:S(2)}, u32[]{:S(2)}) collective-permute-start(bf16[704,256]{1,0:T(8,128)(2,1)} %copy-done.19), channel_id=1, source_target_pairs={{0,4},{1,5},{2,6},{3,7},{4,12},{5,13},{6,14},{7,15},{8,0},{9,1},{1... | collective-permute-start | bytes 1081352 | tf_op jit(solution)/shard_map/ppermute | solution.py:21
  324.1 31.5 %collective-permute-start.66 = (bf16[704,384]{1,0:T(8,128)(2,1)S(1)}, bf16[704,384]{1,0:T(8,128)(2,1)S(1)}, u32[]{:S(2)}, u32[]{:S(2)}) collective-permute-start(bf16[704,384]{1,0:T(8,128)(2,1)S(1)} %collective-permute-done.65.refs_18_.refs_26_.refs_30_), channel_id=1, source_target_pairs={{0,8},{1,9},{2,10},{3,11},{4,0},{5,1},{6,2},{7,3},{8,16},{9,17},{1... | collective-permute-start | bytes 1622024 | tf_op jit(solution)/shard_map/ppermute | solution.py:21
  326.1 31.3 %collective-permute-start.63 = (bf16[704,384]{1,0:T(8,128)(2,1)S(1)}, bf16[704,384]{1,0:T(8,128)(2,1)S(1)}, u32[]{:S(2)}, u32[]{:S(2)}) collective-permute-start(bf16[704,384]{1,0:T(8,128)(2,1)S(1)} %collective-permute-done.62.refs_17_.refs_23_.refs_26_), channel_id=1, source_target_pairs={{0,4},{1,5},{2,6},{3,7},{4,12},{5,13},{6,14},{7,15},{8,0},{9,1},{1... | collective-permute-start | bytes 1622024 | tf_op jit(solution)/shard_map/ppermute | solution.py:21
  (106 other events, 2700.1 us)

commit v2 on v1

--- a/solution.py
+++ b/solution.py
@@ -11,6 +11,7 @@
 STRIPES = 8
 SIDES = 2
 PLACES = STRIPES // SIDES
+PARTS = 2
 TOP, LOW, TURN = STRIPES, STRIPES + 1, STRIPES + 2
 VMEM = 60 * 2**20
 
@@ -345,7 +346,8 @@
         for index, (start, end) in enumerate(cuts):
             chunk = dressed[:, start:end]
             gathered.append(ring_gather(chunk, band_size, index == part % 2))
-            beside.append(across_gather(chunk, band_size))
+            last = part == PARTS - 1
+            beside.append(across_gather(chunk, band_size) if last else None)
         bands.append(band_gather(dressed, levels))
     band = join_band(bands, column)
 
@@ -358,10 +360,11 @@
     for turn in range(PLACES):
         chunks, keys = [], []
         for pieces, other in zip(gathered, beside):
-            reach = [d for d in range(STRIPES) if min(d, STRIPES - d) <= turn + 1]
+            steps = turn + 1 if other is not None else max(turn + 1, PLACES - 1)
+            reach = [d for d in range(STRIPES) if min(d, STRIPES - d) <= steps]
             chunk = [pieces[d] for d in reach]
             names = [(d,) for d in reach]
-            if turn == 0:
+            if turn == 0 and other is not None:
                 chunk.append(other)
                 names.append((3, 5))
             chunks.append(chunk)

time: 400 us -> 395 us (0.988)
    ppermute x72 -> x70, starting transfers between devices: 92.3 us -> 89.7 us  [send(): lax.ppermute(value, 'tri', [pair for pair in pairs if pair[1] is not None])]
    ppermute x72 -> x70, waiting for transfers between devices: 135 us -> 133 us  [send(): lax.ppermute(value, 'tri', [pair for pair in pairs if pair[1] is not None])]
  transfers between devices with their start and end apart: 72 -> 70, of which waited for: 31 -> 33; matrix products, arithmetic and copies ran while one was open for 2% -> 2% of each run, Pallas kernels for 34% -> 35%
where the time goes in v2:
time: 395 us; the launch traced here: 394 us
  Pallas kernels  155 us (39%)
  waiting for transfers between devices  133 us (34%)
  starting transfers between devices  89.7 us (23%)
  local copies, waits for them, and re-layouts  12.3 us (3%)
    ppermute x70, waiting for transfers between devices, send(): lax.ppermute(value, 'tri', [pair for pair in pairs if pair[1] is not None])  133 us
    ppermute x70, starting transfers between devices, send(): lax.ppermute(value, 'tri', [pair for pair in pairs if pair[1] is not None])  89.7 us
    pallas_call x4, Pallas kernels, update(): pl.pallas_call(functools.partial(update_kernel, rows, turn, spans, keys,...  74.7 us
    pallas_call x4, Pallas kernels, image_terms(): pl.pallas_call(functools.partial(terms_kernel, rows, steps, spans), out_s...  74.5 us
  transfers between devices with their start and end apart: 70, of which 33 were waited for; matrix products, arithmetic and copies ran while one was open for 2% of the time, Pallas kernels for 35%

profile of v2, /device:TPU:0, one launch (start us, length us, event | category | flops | bytes accessed | tf_op | source)
XLA Modules:
  0.0 394.3 jit_solution(15317887585076100767)
XLA Ops:
  17.1 15.7 %collective-permute-done.3.refs_7_ = bf16[704,256]{1,0:T(8,128)(2,1)S(1)} collective-permute-done((bf16[704,256]{1,0:T(8,128)(2,1)S(1)}, bf16[704,256]{1,0:T(8,128)(2,1)S(1)}, u32[]{:S(2)}, u32[]{:S(2)}) %collective-permute-start.3) | collective-permute-done | bytes 360480 | tf_op jit(solution)/shard_map/ppermute | solution.py:22
  37.1 7.4 %collective-permute-done.24.refs_7_ = bf16[704,384]{1,0:T(8,128)(2,1)} collective-permute-done((bf16[704,384]{1,0:T(8,128)(2,1)S(1)}, bf16[704,384]{1,0:T(8,128)(2,1)}, u32[]{:S(2)}, u32[]{:S(2)}) %collective-permute-start.24) | collective-permute-done | bytes 540704 | tf_op jit(solution)/shard_map/ppermute | solution.py:22
  46.5 5.6 %collective-permute-done.12.refs_14_ = bf16[704,256]{1,0:T(8,128)(2,1)S(1)} collective-permute-done((bf16[704,256]{1,0:T(8,128)(2,1)S(1)}, bf16[704,256]{1,0:T(8,128)(2,1)S(1)}, u32[]{:S(2)}, u32[]{:S(2)}) %collective-permute-start.12) | collective-permute-done | bytes 360480 | tf_op jit(solution)/shard_map/ppermute | solution.py:22
  80.9 6.1 %collective-permute-done.31.refs_14_ = bf16[704,384]{1,0:T(8,128)(2,1)} collective-permute-done((bf16[704,384]{1,0:T(8,128)(2,1)S(1)}, bf16[704,384]{1,0:T(8,128)(2,1)}, u32[]{:S(2)}, u32[]{:S(2)}) %collective-permute-start.31) | collective-permute-done | bytes 540704 | tf_op jit(solution)/shard_map/ppermute | solution.py:22
  92.6 5.9 %collective-permute-done.25.refs_6_ = bf16[704,384]{1,0:T(8,128)(2,1)} collective-permute-done((bf16[704,384]{1,0:T(8,128)(2,1)}, bf16[704,384]{1,0:T(8,128)(2,1)}, u32[]{:S(2)}, u32[]{:S(2)}) %collective-permute-start.25) | collective-permute-done | bytes 540704 | tf_op jit(solution)/shard_map/ppermute | solution.py:22
  104.2 5.7 %collective-permute-done.10.refs_12_ = bf16[704,256]{1,0:T(8,128)(2,1)} collective-permute-done((bf16[704,256]{1,0:T(8,128)(2,1)}, bf16[704,256]{1,0:T(8,128)(2,1)}, u32[]{:S(2)}, u32[]{:S(2)}) %collective-permute-start.10) | collective-permute-done | bytes 360480 | tf_op jit(solution)/shard_map/ppermute | solution.py:22
  111.9 16.1 %shard_map.47 = (bf16[1,704,512]{2,1,0:T(8,128)(2,1)}, bf16[1,704,512]{2,1,0:T(8,128)(2,1)}) custom-call(s32[22]{0:T(128)} %stack.91.where_ref, bf16[1,2816,5632]{2,1,0:T(8,128)(2,1)} %tile_ref.7, bf16[704,256]{1,0:T(8,128)(2,1)} %copy-done.24, bf16[704,256]{1,0:T(8,128)(2,1)} %copy-done.32, bf16[704,256]{1,0:T(8,128)(2,1)} %copy-done.36, ...), custom_call_target="tpu_custom_call" | custom-call | flops 8120172544 | bytes 15859712 | tf_op jit(solution)/shard_map/pallas_call | solution.py:130
  131.9 16.0 %shard_map.46 = (bf16[1,704,512]{2,1,0:T(8,128)(2,1)}, bf16[1,704,512]{2,1,0:T(8,128)(2,1)}) custom-call(s32[22]{0:T(128)} %stack.91.where_ref, bf16[1,2816,5632]{2,1,0:T(8,128)(2,1)} %tile_ref.7, bf16[704,256]{1,0:T(8,128)(2,1)} %copy-done.24, bf16[704,256]{1,0:T(8,128)(2,1)} %copy-done.32, bf16[704,256]{1,0:T(8,128)(2,1)} %copy-done.36, ...), custom_call_target="tpu_custom_call" | custom-call | flops 8120172544 | bytes 15859712 | tf_op jit(solution)/shard_map/pallas_call | solution.py:130
  151.4 21.2 %shard_map.49 = (bf16[1,704,768]{2,1,0:T(8,128)(2,1)}, bf16[1,704,768]{2,1,0:T(8,128)(2,1)}) custom-call(s32[22]{0:T(128)} %stack.91.where_ref, bf16[1,2816,5632]{2,1,0:T(8,128)(2,1)} %tile_ref.7, bf16[704,384]{1,0:T(8,128)(2,1)} %copy-done.52, bf16[704,384]{1,0:T(8,128)(2,1)} %collective-permute-done.20.refs_1_, ...), custom_call_target="tpu_custom_call" | custom-call | flops 12180258816 | bytes 15859712 | tf_op jit(solution)/shard_map/pallas_call | solution.py:130
  172.9 21.3 %shard_map.48 = (bf16[1,704,768]{2,1,0:T(8,128)(2,1)}, bf16[1,704,768]{2,1,0:T(8,128)(2,1)}) custom-call(s32[22]{0:T(128)} %stack.91.where_ref, bf16[1,2816,5632]{2,1,0:T(8,128)(2,1)} %tile_ref.7, bf16[704,384]{1,0:T(8,128)(2,1)} %copy-done.52, bf16[704,384]{1,0:T(8,128)(2,1)} %collective-permute-done.20.refs_1_, ...), custom_call_target="tpu_custom_call" | custom-call | flops 12180258816 | bytes 15859712 | tf_op jit(solution)/shard_map/pallas_call | solution.py:130
  199.1 8.7 %collective-permute-done.51.refs_13_.refs_15_ = bf16[704,256]{1,0:T(8,128)(2,1)S(1)} collective-permute-done((bf16[704,256]{1,0:T(8,128)(2,1)S(1)}, bf16[704,256]{1,0:T(8,128)(2,1)S(1)}, u32[]{:S(2)}, u32[]{:S(2)}) %collective-permute-start.51) | collective-permute-done | bytes 360480 | tf_op jit(solution)/shard_map/ppermute | solution.py:22
  210.2 4.8 %collective-permute-done.43.refs_6_.refs_7_ = bf16[704,256]{1,0:T(8,128)(2,1)S(1)} collective-permute-done((bf16[704,256]{1,0:T(8,128)(2,1)S(1)}, bf16[704,256]{1,0:T(8,128)(2,1)S(1)}, u32[]{:S(2)}, u32[]{:S(2)}) %collective-permute-start.43) | collective-permute-done | bytes 360480 | tf_op jit(solution)/shard_map/ppermute | solution.py:22
  215.5 5.9 %collective-permute-done.36 = bf16[704,768]{1,0:T(8,128)(2,1)S(1)} collective-permute-done((bf16[704,768]{1,0:T(8,128)(2,1)S(1)}, bf16[704,768]{1,0:T(8,128)(2,1)S(1)}, u32[]{:S(2)}, u32[]{:S(2)}) %collective-permute-start.36) | collective-permute-done | bytes 1081376 | tf_op jit(solution)/shard_map/ppermute | solution.py:22
  226.3 4.3 %collective-permute-done.48.refs_9_.refs_10_ = bf16[704,256]{1,0:T(8,128)(2,1)S(1)} collective-permute-done((bf16[704,256]{1,0:T(8,128)(2,1)S(1)}, bf16[704,256]{1,0:T(8,128)(2,1)S(1)}, u32[]{:S(2)}, u32[]{:S(2)}) %collective-permute-start.48) | collective-permute-done | bytes 360480 | tf_op jit(solution)/shard_map/ppermute | solution.py:22
  242.8 4.2 %collective-permute-done.53.refs_11_.refs_13_ = bf16[704,256]{1,0:T(8,128)(2,1)S(1)} collective-permute-done((bf16[704,256]{1,0:T(8,128)(2,1)S(1)}, bf16[704,256]{1,0:T(8,128)(2,1)S(1)}, u32[]{:S(2)}, u32[]{:S(2)}) %collective-permute-start.53) | collective-permute-done | bytes 360480 | tf_op jit(solution)/shard_map/ppermute | solution.py:22
  261.1 4.0 %collective-permute-start.58 = (bf16[704,384]{1,0:T(8,128)(2,1)S(1)}, bf16[704,384]{1,0:T(8,128)(2,1)}, u32[]{:S(2)}, u32[]{:S(2)}) collective-permute-start(bf16[704,384]{1,0:T(8,128)(2,1)S(1)} %get-tuple-element.26.refs_14_.refs_16_), channel_id=1, source_target_pairs={{0,8},{1,9},{2,10},{3,11},{4,0},{5,1},{6,2},{7,3},{8,16},{9,17},{1... | collective-permute-start | bytes 1622024 | tf_op jit(solution)/shard_map/ppermute | solution.py:22
  266.8 7.9 %collective-permute-done.61.refs_19_.refs_20_.refs_22_.refs_25_ = bf16[704,384]{1,0:T(8,128)(2,1)S(1)} collective-permute-done((bf16[704,384]{1,0:T(8,128)(2,1)S(1)}, bf16[704,384]{1,0:T(8,128)(2,1)S(1)}, u32[]{:S(2)}, u32[]{:S(2)}) %collective-permute-start.61) | collective-permute-done | bytes 540704 | tf_op jit(solution)/shard_map/ppermute | solution.py:22
  279.8 6.0 %collective-permute-done.54.refs_15_.refs_17_ = bf16[704,384]{1,0:T(8,128)(2,1)} collective-permute-done((bf16[704,384]{1,0:T(8,128)(2,1)S(1)}, bf16[704,384]{1,0:T(8,128)(2,1)}, u32[]{:S(2)}, u32[]{:S(2)}) %collective-permute-start.54) | collective-permute-done | bytes 540704 | tf_op jit(solution)/shard_map/ppermute | solution.py:22
  294.5 6.1 %shard_map.50.band_ref = bf16[2816,1280]{1,0:T(8,128)(2,1)} custom-call(s32[1]{0:T(128)} %bitcast.22.column_ref, bf16[704,512]{1,0:T(8,128)(2,1)} %copy-done.8, bf16[704,512]{1,0:T(8,128)(2,1)} %copy-done.47, bf16[704,512]{1,0:T(8,128)(2,1)} %copy-done.46, bf16[704,512]{1,0:T(8,128)(2,1)} %copy-done.48, bf16[704,768]{1,0:T(8,128)(2,1)} %copy-done.2, ...), custom_call_target="tpu_custom_call" | custom-call | flops 1073741824 | bytes 14417920 | tf_op jit(solution)/shard_map/pallas_call | solution.py:199
  304.9 7.8 %collective-permute-done.55.refs_16_.refs_18_ = bf16[704,384]{1,0:T(8,128)(2,1)} collective-permute-done((bf16[704,384]{1,0:T(8,128)(2,1)}, bf16[704,384]{1,0:T(8,128)(2,1)}, u32[]{:S(2)}, u32[]{:S(2)}) %collective-permute-start.55) | collective-permute-done | bytes 540704 | tf_op jit(solution)/shard_map/ppermute | solution.py:22
  314.3 18.6 %shard_map.51.refs_26_ = f32[1,2816,5632]{2,1,0:T(8,128)} custom-call(s32[22]{0:T(128)} %stack.91.where_ref, bf16[2816,1280]{1,0:T(8,128)(2,1)} %shard_map.50.band_ref, bf16[704,256]{1,0:T(8,128)(2,1)} %copy-done.4, bf16[704,256]{1,0:T(8,128)(2,1)} %copy-done.12, bf16[704,256]{1,0:T(8,128)(2,1)} %copy-done.16, bf16[704,256]{1,0:T(8,128)(2,1)} %copy-done.22, ...), custom_call_target="tpu_custom_call" | custom-call | flops 10150215680 | bytes 15859712 | tf_op jit(solution)/shard_map/pallas_call | solution.py:275
  332.9 18.8 %shard_map.52.refs_30_ = f32[1,2816,5632]{2,1,0:T(8,128)} custom-call(s32[22]{0:T(128)} %stack.91.where_ref, bf16[2816,1280]{1,0:T(8,128)(2,1)} %shard_map.50.band_ref, bf16[704,256]{1,0:T(8,128)(2,1)} %copy-done.4, bf16[704,256]{1,0:T(8,128)(2,1)} %copy-done.12, bf16[704,256]{1,0:T(8,128)(2,1)} %copy-done.16, ...), custom_call_target="tpu_custom_call", output_to_operand_aliasing={{}: (28, {})} | custom-call | flops 10150215680 | bytes 15859712 | tf_op jit(solution)/shard_map/pallas_call | solution.py:275
  355.2 18.6 %shard_map.53.refs_34_ = f32[1,2816,5632]{2,1,0:T(8,128)} custom-call(s32[22]{0:T(128)} %stack.91.where_ref, bf16[2816,1280]{1,0:T(8,128)(2,1)} %shard_map.50.band_ref, bf16[704,256]{1,0:T(8,128)(2,1)} %copy-done.4, bf16[704,256]{1,0:T(8,128)(2,1)} %copy-done.12, bf16[704,256]{1,0:T(8,128)(2,1)} %copy-done.16, ...), custom_call_target="tpu_custom_call", output_to_operand_aliasing={{}: (32, {})} | custom-call | flops 10150215680 | bytes 15859712 | tf_op jit(solution)/shard_map/pallas_call | solution.py:275
  375.5 18.6 %shard_map.54 = f32[1,2816,5632]{2,1,0:T(8,128)} custom-call(s32[22]{0:T(128)} %stack.91.where_ref, bf16[2816,1280]{1,0:T(8,128)(2,1)} %shard_map.50.band_ref, bf16[704,256]{1,0:T(8,128)(2,1)} %copy-done.4, bf16[704,256]{1,0:T(8,128)(2,1)} %copy-done.12, bf16[704,256]{1,0:T(8,128)(2,1)} %copy-done.16, ...), custom_call_target="tpu_custom_call", output_to_operand_aliasing={{}: (36, {})} | custom-call | flops 10150215680 | bytes 15859712 | tf_op jit(solution)/shard_map/pallas_call | solution.py:275
  (256 shorter events, 137.6 us)
Async XLA Ops:
  5.6 29.4 %collective-permute-start.30 = (bf16[704,384]{1,0:T(8,128)(2,1)S(1)}, bf16[704,384]{1,0:T(8,128)(2,1)S(1)}, u32[]{:S(2)}, u32[]{:S(2)}) collective-permute-start(bf16[704,384]{1,0:T(8,128)(2,1)S(1)} %get-tuple-element.21.refs_8_), channel_id=1, source_target_pairs={{0,8},{1,9},{2,10},{3,11},{4,0},{5,1},{6,2},{7,3},{8,16},{9,17},{1... | collective-permute-start | bytes 1622024 | tf_op jit(solution)/shard_map/ppermute | solution.py:22
  7.7 29.2 %collective-permute-start.27 = (bf16[704,384]{1,0:T(8,128)(2,1)S(1)}, bf16[704,384]{1,0:T(8,128)(2,1)}, u32[]{:S(2)}, u32[]{:S(2)}) collective-permute-start(bf16[704,384]{1,0:T(8,128)(2,1)S(1)} %get-tuple-element.21.refs_8_), channel_id=1, source_target_pairs={{0,4},{1,5},{2,6},{3,7},{4,12},{5,13},{6,14},{7,15},{8,0},{9,1},{1... | collective-permute-start | bytes 1622024 | tf_op jit(solution)/shard_map/ppermute | solution.py:22
  15.6 28.9 %collective-permute-start.24 = (bf16[704,384]{1,0:T(8,128)(2,1)S(1)}, bf16[704,384]{1,0:T(8,128)(2,1)}, u32[]{:S(2)}, u32[]{:S(2)}) collective-permute-start(bf16[704,384]{1,0:T(8,128)(2,1)S(1)} %get-tuple-element.22.refs_0_), channel_id=1, source_target_pairs={{0,8},{1,9},{2,10},{3,11},{4,0},{5,1},{6,2},{7,3},{8,16},{9,17},{1... | collective-permute-start | bytes 1622024 | tf_op jit(solution)/shard_map/ppermute | solution.py:22
  32.8 29.1 %collective-permute-start.20 = (bf16[704,384]{1,0:T(8,128)(2,1)S(1)}, bf16[704,384]{1,0:T(8,128)(2,1)}, u32[]{:S(2)}, u32[]{:S(2)}) collective-permute-start(bf16[704,384]{1,0:T(8,128)(2,1)S(1)} %get-tuple-element.22.refs_0_), channel_id=1, source_target_pairs={{0,4},{1,5},{2,6},{3,7},{4,12},{5,13},{6,14},{7,15},{8,0},{9,1},{1... | collective-permute-start | bytes 1622024 | tf_op jit(solution)/shard_map/ppermute | solution.py:22
  71.3 27.3 %collective-permute-start.25 = (bf16[704,384]{1,0:T(8,128)(2,1)}, bf16[704,384]{1,0:T(8,128)(2,1)}, u32[]{:S(2)}, u32[]{:S(2)}) collective-permute-start(bf16[704,384]{1,0:T(8,128)(2,1)} %collective-permute-done.24.refs_7_), channel_id=1, source_target_pairs={{0,8},{1,9},{2,10},{3,11},{4,0},{5,1},{6,2},{7,3},{8,16},{9,17},{1... | collective-permute-start | bytes 1622024 | tf_op jit(solution)/shard_map/ppermute | solution.py:22
  75.4 26.8 %collective-permute-start.21 = (bf16[704,384]{1,0:T(8,128)(2,1)}, bf16[704,384]{1,0:T(8,128)(2,1)}, u32[]{:S(2)}, u32[]{:S(2)}) collective-permute-start(bf16[704,384]{1,0:T(8,128)(2,1)} %collective-permute-done.20.refs_1_), channel_id=1, source_target_pairs={{0,4},{1,5},{2,6},{3,7},{4,12},{5,13},{6,14},{7,15},{8,0},{9,1},{1... | collective-permute-start | bytes 1622024 | tf_op jit(solution)/shard_map/ppermute | solution.py:22
  78.9 31.0 %collective-permute-start.10 = (bf16[704,256]{1,0:T(8,128)(2,1)}, bf16[704,256]{1,0:T(8,128)(2,1)}, u32[]{:S(2)}, u32[]{:S(2)}) collective-permute-start(bf16[704,256]{1,0:T(8,128)(2,1)} %collective-permute-done.9.refs_11_), channel_id=1, source_target_pairs={{0,4},{1,5},{2,6},{3,7},{4,12},{5,13},{6,14},{7,15},{8,0},{9,1},{1... | collective-permute-start | bytes 1081352 | tf_op jit(solution)/shard_map/ppermute | solution.py:22
  90.6 37.5 %collective-permute-start.32 = (bf16[704,384]{1,0:T(8,128)(2,1)}, bf16[704,384]{1,0:T(8,128)(2,1)}, u32[]{:S(2)}, u32[]{:S(2)}) collective-permute-start(bf16[704,384]{1,0:T(8,128)(2,1)} %collective-permute-done.31.refs_14_), channel_id=1, source_target_pairs={{0,8},{1,9},{2,10},{3,11},{4,0},{5,1},{6,2},{7,3},{8,16},{9,17},{1... | collective-permute-start | bytes 1622024 | tf_op jit(solution)/shard_map/ppermute | solution.py:22
  98.6 50.6 %collective-permute-start.29 = (bf16[704,384]{1,0:T(8,128)(2,1)}, bf16[704,384]{1,0:T(8,128)(2,1)}, u32[]{:S(2)}, u32[]{:S(2)}) collective-permute-start(bf16[704,384]{1,0:T(8,128)(2,1)} %collective-permute-done.28.refs_10_), channel_id=1, source_target_pairs={{0,4},{1,5},{2,6},{3,7},{4,12},{5,13},{6,14},{7,15},{8,0},{9,1},{1... | collective-permute-start | bytes 1622024 | tf_op jit(solution)/shard_map/ppermute | solution.py:22
  102.2 48.4 %collective-permute-start.26 = (bf16[704,384]{1,0:T(8,128)(2,1)}, bf16[704,384]{1,0:T(8,128)(2,1)}, u32[]{:S(2)}, u32[]{:S(2)}) collective-permute-start(bf16[704,384]{1,0:T(8,128)(2,1)} %collective-permute-done.25.refs_6_), channel_id=1, source_target_pairs={{0,8},{1,9},{2,10},{3,11},{4,0},{5,1},{6,2},{7,3},{8,16},{9,17},{1... | collective-permute-start | bytes 1622024 | tf_op jit(solution)/shard_map/ppermute | solution.py:22
  148.0 47.3 %collective-permute-start.14 = (bf16[1,704,512]{2,1,0:T(8,128)(2,1)}, bf16[1,704,512]{2,1,0:T(8,128)(2,1)S(1)}, u32[]{:S(2)}, u32[]{:S(2)}) collective-permute-start(bf16[1,704,512]{2,1,0:T(8,128)(2,1)} %get-tuple-element.14), channel_id=1, source_target_pairs={{0,1},{1,0},{2,3},{3,2},{4,5},{5,4},{6,7},{7,6},{8,9},{9,8},{10,11... | collective-permute-start | bytes 2162696 | tf_op jit(solution)/shard_map/ppermute | solution.py:22
  149.1 46.2 %collective-permute-start.16 = (bf16[704,512]{1,0:T(8,128)(2,1)}, bf16[704,512]{1,0:T(8,128)(2,1)S(1)}, u32[]{:S(2)}, u32[]{:S(2)}) collective-permute-start(bf16[704,512]{1,0:T(8,128)(2,1)} %fusion.5), channel_id=1, source_target_pairs={{0,2},{1,3},{2,0},{3,1},{4,6},{5,7},{6,4},{7,5},{8,10},{9,11},{10,... | collective-permute-start | bytes 2162696 | tf_op jit(solution)/shard_map/ppermute | solution.py:22
  194.7 26.8 %collective-permute-start.36 = (bf16[704,768]{1,0:T(8,128)(2,1)S(1)}, bf16[704,768]{1,0:T(8,128)(2,1)S(1)}, u32[]{:S(2)}, u32[]{:S(2)}) collective-permute-start(bf16[704,768]{1,0:T(8,128)(2,1)S(1)} %fusion.4), channel_id=1, source_target_pairs={{0,2},{1,3},{2,0},{3,1},{4,6},{5,7},{6,4},{7,5},{8,10},{9,11},{10,... | collective-permute-start | bytes 3244040 | tf_op jit(solution)/shard_map/ppermute | solution.py:22
  209.5 31.4 %collective-permute-start.18 = (bf16[704,512]{1,0:T(8,128)(2,1)S(1)}, bf16[704,512]{1,0:T(8,128)(2,1)S(1)}, u32[]{:S(2)}, u32[]{:S(2)}) collective-permute-start(bf16[704,512]{1,0:T(8,128)(2,1)S(1)} %fusion.3.refs_0_), channel_id=1, source_target_pairs={{0,2},{1,3},{2,0},{3,1},{4,6},{5,7},{6,4},{7,5},{8,10},{9,11},{10,... | collective-permute-start | bytes 2162696 | tf_op jit(solution)/shard_map/ppermute | solution.py:22
  215.0 26.3 %collective-permute-start.17 = (bf16[704,512]{1,0:T(8,128)(2,1)S(1)}, bf16[704,512]{1,0:T(8,128)(2,1)S(1)}, u32[]{:S(2)}, u32[]{:S(2)}) collective-permute-start(bf16[704,512]{1,0:T(8,128)(2,1)S(1)} %fusion.3.refs_0_), channel_id=1, source_target_pairs={{0,1},{1,0},{2,3},{3,2},{4,5},{5,4},{6,7},{7,6},{8,9},{9,8},{10,11... | collective-permute-start | bytes 2162696 | tf_op jit(solution)/shard_map/ppermute | solution.py:22
  223.7 35.8 %collective-permute-start.38 = (bf16[704,768]{1,0:T(8,128)(2,1)S(1)}, bf16[704,768]{1,0:T(8,128)(2,1)S(1)}, u32[]{:S(2)}, u32[]{:S(2)}) collective-permute-start(bf16[704,768]{1,0:T(8,128)(2,1)S(1)} %fusion.1.refs_4_), channel_id=1, source_target_pairs={{0,2},{1,3},{2,0},{3,1},{4,6},{5,7},{6,4},{7,5},{8,10},{9,11},{10,... | collective-permute-start | bytes 3244040 | tf_op jit(solution)/shard_map/ppermute | solution.py:22
  255.7 31.8 %collective-permute-start.37 = (bf16[704,768]{1,0:T(8,128)(2,1)S(1)}, bf16[704,768]{1,0:T(8,128)(2,1)S(1)}, u32[]{:S(2)}, u32[]{:S(2)}) collective-permute-start(bf16[704,768]{1,0:T(8,128)(2,1)S(1)} %fusion.1.refs_4_), channel_id=1, source_target_pairs={{0,1},{1,0},{2,3},{3,2},{4,5},{5,4},{6,7},{7,6},{8,9},{9,8},{10,11... | collective-permute-start | bytes 3244040 | tf_op jit(solution)/shard_map/ppermute | solution.py:22
  259.5 28.5 %collective-permute-start.39 = (bf16[704,768]{1,0:T(8,128)(2,1)S(1)}, bf16[704,768]{1,0:T(8,128)(2,1)S(1)}, u32[]{:S(2)}, u32[]{:S(2)}) collective-permute-start(bf16[704,768]{1,0:T(8,128)(2,1)S(1)} %collective-permute-done.38.refs_6_), channel_id=1, source_target_pairs={{0,1},{1,0},{2,3},{3,2},{4,5},{5,4},{6,7},{7,6},{8,9},{9,8},{10,11... | collective-permute-start | bytes 3244040 | tf_op jit(solution)/shard_map/ppermute | solution.py:22
  276.3 26.1 %collective-permute-start.65 = (bf16[704,384]{1,0:T(8,128)(2,1)S(1)}, bf16[704,384]{1,0:T(8,128)(2,1)}, u32[]{:S(2)}, u32[]{:S(2)}) collective-permute-start(bf16[704,384]{1,0:T(8,128)(2,1)S(1)} %collective-permute-done.64.refs_20_.refs_23_.refs_27_.refs_31_), channel_id=1, source_target_pairs={{0,8},{1,9},{2,10},{3,11},{4,0},{5,1},{6,2},{7,3},{8,16},{9,17},{1... | collective-permute-start | bytes 1622024 | tf_op jit(solution)/shard_map/ppermute | solution.py:22
  300.7 73.1 %collective-permute-start.50 = (bf16[704,256]{1,0:T(8,128)(2,1)S(1)}, bf16[704,256]{1,0:T(8,128)(2,1)}, u32[]{:S(2)}, u32[]{:S(2)}) collective-permute-start(bf16[704,256]{1,0:T(8,128)(2,1)S(1)} %copy-done.19), channel_id=1, source_target_pairs={{0,4},{1,5},{2,6},{3,7},{4,12},{5,13},{6,14},{7,15},{8,0},{9,1},{1... | collective-permute-start | bytes 1081352 | tf_op jit(solution)/shard_map/ppermute | solution.py:22
  302.3 49.4 %collective-permute-start.66 = (bf16[704,384]{1,0:T(8,128)(2,1)}, bf16[704,384]{1,0:T(8,128)(2,1)S(1)}, u32[]{:S(2)}, u32[]{:S(2)}) collective-permute-start(bf16[704,384]{1,0:T(8,128)(2,1)} %collective-permute-done.65.refs_22_.refs_26_.refs_30_), channel_id=1, source_target_pairs={{0,8},{1,9},{2,10},{3,11},{4,0},{5,1},{6,2},{7,3},{8,16},{9,17},{1... | collective-permute-start | bytes 1622024 | tf_op jit(solution)/shard_map/ppermute | solution.py:22
  302.8 49.5 %collective-permute-start.63 = (bf16[704,384]{1,0:T(8,128)(2,1)}, bf16[704,384]{1,0:T(8,128)(2,1)S(1)}, u32[]{:S(2)}, u32[]{:S(2)}) collective-permute-start(bf16[704,384]{1,0:T(8,128)(2,1)} %collective-permute-done.62.refs_21_.refs_23_.refs_26_), channel_id=1, source_target_pairs={{0,4},{1,5},{2,6},{3,7},{4,12},{5,13},{6,14},{7,15},{8,0},{9,1},{1... | collective-permute-start | bytes 1622024 | tf_op jit(solution)/shard_map/ppermute | solution.py:22
  304.4 50.0 %collective-permute-start.60 = (bf16[704,384]{1,0:T(8,128)(2,1)}, bf16[704,384]{1,0:T(8,128)(2,1)S(1)}, u32[]{:S(2)}, u32[]{:S(2)}) collective-permute-start(bf16[704,384]{1,0:T(8,128)(2,1)} %collective-permute-done.59.refs_17_.refs_19_.refs_22_), channel_id=1, source_target_pairs={{0,8},{1,9},{2,10},{3,11},{4,0},{5,1},{6,2},{7,3},{8,16},{9,17},{1... | collective-permute-start | bytes 1622024 | tf_op jit(solution)/shard_map/ppermute | solution.py:22
  312.7 40.1 %collective-permute-start.56 = (bf16[704,384]{1,0:T(8,128)(2,1)}, bf16[704,384]{1,0:T(8,128)(2,1)S(1)}, u32[]{:S(2)}, u32[]{:S(2)}) collective-permute-start(bf16[704,384]{1,0:T(8,128)(2,1)} %collective-permute-done.55.refs_16_.refs_18_), channel_id=1, source_target_pairs={{0,4},{1,5},{2,6},{3,7},{4,12},{5,13},{6,14},{7,15},{8,0},{9,1},{1... | collective-permute-start | bytes 1622024 | tf_op jit(solution)/shard_map/ppermute | solution.py:22
  (104 other events, 2938.5 us)
